TPU v7x, 128 devices: a whole 4x4x4 slice. The times are simulated.
128 devices in a mesh: gx: 8 (over z_lo, y), gy: 16 (over x, z_hi, core).
Axes of the slice: x: 4, y: 4, z: 4 (z_hi: 2, z_lo: 2; z = z_hi * 2 + z_lo), core: 2. Of those that a mesh axis runs over, the one named last changes fastest.
Arguments:
- cotangent: float32 [256, 1024, 128], P('gx', 'gy'), may hold values from -6 to 6
- speed: float32 [3, 256, 1024, 128], P(None, 'gx', 'gy'), may hold values from 0.05 to 0.45
- coeff: float32 [3, 256, 1024, 128], P(None, 'gx', 'gy'), may hold values from 0.3 to 3
- dirs: int32 [3, 256, 1024], P(None, 'gx', 'gy'), may hold values from 0 to 1
Outputs:
- grad: float32 [256, 1024, 128], P('gx', 'gy')
Inputs may be any that keep to these rules, and one draw needn't show every extreme that they name: `dirs`: 0 means the lower cell of a face is upwind, 1 the upper cell.
All inputs are finite; a program needn't handle non-finite values.
Results may differ from a plain program's by a relative error of at most 0.0003.
Values sent between devices are 32-bit elements; how exact they have to be, the bound alone decides.
A program may use at most 128 MiB of HBM per device.

v0:
```python
import jax
import jax.numpy as jnp
from jax import lax
from jax.sharding import Mesh
from jax.sharding import PartitionSpec as P

ITERS = 2
GX_GY = ("gx_0", "gx_1", "gy_0", "gy_1", "gy_2")
GX = ("gx_0", "gx_1")
GY = ("gy_0", "gy_1", "gy_2")


explicit_table = (
    (0.0, 0.0, 0.0, 0.0),
    (0.5, 0.0, 0.0, 0.0),
    (0.25, 0.5, 0.0, 0.0),
    (0.2, 0.3, 0.5, 0.0),
)
implicit_table = (
    (0.0, 0.0, 0.0, 0.0),
    (0.25, 0.25, 0.0, 0.0),
    (0.25, 0.25, 0.25, 0.0),
    (0.15, 0.35, 0.25, 0.25),
)
section_weights = (0.15, 0.35, 0.25, 0.25)
implicit_diagonal = 0.25
step_length = 1.0


def padded(array, sides, width):
    edges = {}
    for axis, dim in sides:
        size, length = (lax.axis_size(axis), array.shape[dim])
        up = [(i, (i + 1) % size) for i in range(size - 1)]
        last = lax.slice_in_dim(array, length - width, length, axis=dim)
        leading = lax.slice_in_dim(array, 0, width, axis=dim)
        edges[dim] = (
            lax.ppermute(last, axis, up),
            lax.ppermute(leading, axis, [(b, a) for a, b in up]),
        )
    done = []
    for _, dim in sides:
        low, high = edges[dim]
        around = [(width, width) if d in done else (0, 0) for d in range(array.ndim)]
        array = jnp.concatenate([jnp.pad(low, around), array, jnp.pad(high, around)], axis=dim)
        done.append(dim)
    return array


def by_axis(array, axes):
    for axis in axes:
        array = lax.psum(array, axis)
    return array


def passed_along(value, axis, steps):
    count = lax.axis_size(axis)
    leading, last = (max(0, -steps), min(count, count - steps))
    return lax.ppermute(value, axis, [(source, source + steps) for source in range(leading, last)])


def local_ahead(values, dimension):
    tail = lax.slice_in_dim(values, 1, values.shape[dimension], axis=dimension)
    return jnp.concatenate(
        [tail, jnp.zeros_like(lax.slice_in_dim(values, 0, 1, axis=dimension))], dimension
    )


def local_behind(values, dimension):
    head = lax.slice_in_dim(values, 0, values.shape[dimension] - 1, axis=dimension)
    return jnp.concatenate(
        [jnp.zeros_like(lax.slice_in_dim(values, 0, 1, axis=dimension)), head], dimension
    )


def with_plane_before(values, plane, dimension):
    head = lax.slice_in_dim(values, 0, values.shape[dimension] - 1, axis=dimension)
    return jnp.concatenate([plane, head], dimension)


def apply_halo(fields, coeff, velocity, coeff_low, velocity_low):
    count = fields.shape[0]
    extended = padded(fields, ((GX, 1), (GY, 2)), 1)
    aheads = (extended[:, 2:, 1:-1], extended[:, 1:-1, 2:], local_ahead(fields, 3))
    behinds = (extended[:, :-2, 1:-1], extended[:, 1:-1, :-2], local_behind(fields, 3))
    diffused = fields[count - 1]
    total = jnp.zeros_like(diffused)
    for dimension in range(3):
        ahead = aheads[dimension]
        behind = behinds[dimension]
        total = total + coeff[dimension] * (ahead[count - 1] - diffused)
        total = total - coeff_low[dimension] * (diffused - behind[count - 1])
        if count == 2:
            moved = velocity[dimension] * (ahead[0] - fields[0])
            total = total + jnp.where(velocity[dimension] > 0, moved, 0.0)
            moved_low = velocity_low[dimension] * (fields[0] - behind[0])
            total = total + jnp.where(velocity_low[dimension] > 0, 0.0, moved_low)
    return total


def paired_products(residual, image):
    return (by_axis(jnp.sum(residual * residual), GX_GY), by_axis(jnp.sum(residual * image), GX_GY))


def local(cotangent, speed, coeff, dirs):
    signs = (1 - 2 * dirs).astype(jnp.float32)
    velocity = speed * signs[..., None]
    rim_x = passed_along(jnp.stack([coeff[0, -1:], velocity[0, -1:]]), GX, 1)
    rim_y = passed_along(jnp.stack([coeff[1, :, -1:], velocity[1, :, -1:]]), GY, 1)
    coeff_low = (
        with_plane_before(coeff[0], rim_x[0], 0),
        with_plane_before(coeff[1], rim_y[0], 1),
        local_behind(coeff[2], 2),
    )
    velocity_low = (
        with_plane_before(velocity[0], rim_x[1], 0),
        with_plane_before(velocity[1], rim_y[1], 1),
        local_behind(velocity[2], 2),
    )

    def operate(fields):
        return apply_halo(fields, coeff, velocity, coeff_low, velocity_low)

    def section_operator(values):
        return values - implicit_diagonal * step_length * operate(values[None])

    section_adjoints = [None, None, None, None]
    for section_index in (3, 2, 1, 0):
        advected = step_length * section_weights[section_index] * cotangent
        diffused = step_length * section_weights[section_index] * cotangent
        for later in range(section_index + 1, 4):
            advected = (
                advected
                + step_length * explicit_table[later][section_index] * section_adjoints[later]
            )
            diffused = (
                diffused
                + step_length * implicit_table[later][section_index] * section_adjoints[later]
            )
        source = operate(jnp.stack([advected, diffused]))
        if section_index > 0:
            solution = jnp.zeros_like(source)
            residual = source
            image = section_operator(residual)
            norm_now, product = paired_products(residual, image)
            alpha = norm_now / product
            direction = residual
            along = image
            for iteration in range(ITERS):
                solution = solution + alpha * direction
                residual = residual - alpha * along
                if iteration + 1 < ITERS:
                    image = section_operator(residual)
                    norm_next, product = paired_products(residual, image)
                    ratio = norm_next / norm_now
                    alpha = norm_next / (product - ratio * norm_next / alpha)
                    direction = residual + ratio * direction
                    along = image + ratio * along
                    norm_now = norm_next
            section_adjoints[section_index] = solution
        else:
            section_adjoints[section_index] = source
    return (
        cotangent
        + section_adjoints[0]
        + section_adjoints[1]
        + section_adjoints[2]
        + section_adjoints[3]
    )


def solution(mesh):
    finer = Mesh(mesh.devices.reshape(2, 4, 4, 2, 2), ("gx_0", "gx_1", "gy_0", "gy_1", "gy_2"))
    placed = (P(GX, GY, None), P(None, GX, GY, None), P(None, GX, GY, None), P(None, GX, GY))
    return jax.shard_map(
        local, mesh=finer, in_specs=placed, out_specs=P(GX, GY, None), check_vma=False
    )
```

profile of v0, /device:TPU:1, one launch (start us, length us, event | category | flops | bytes accessed | tf_op | source)
XLA Modules:
  0.0 487.2 jit_solution(6852311645117691248)
XLA Ops:
  1.5 3.3 collective-permute-start.3
  4.8 5.5 %collective-permute-start.5 = (f32[2,32,1,128]{3,2,1,0:T(1,128)S(1)}, f32[2,32,1,128]{3,2,1,0:T(1,128)S(1)}, u32[]{:S(2)}, u32[]{:S(2)}) collective-permute-start(f32[2,32,1,128]{3,2,1,0:T(1,128)S(1)} %get-tuple-element.149), channel_id=1, source_target_pairs={{0,1},{1,2},{2,3},{3,4},{4,5},{5,6},{6,7},{7,8},{8,9},{9,10},{10,1... | collective-permute-start | bytes 98312 | tf_op jit(solution)/shard_map/ppermute | solution.py:38
  10.3 3.2 collective-permute-start.2
  22.0 4.3 collective-permute-start.1
  29.4 3.8 fusion.9
  35.4 5.1 %collective-permute-start.9 = (f32[1,32,1,128]{3,2,1,0:T(1,128)S(1)}, f32[1,32,1,128]{3,2,1,0:T(1,128)S(1)}, u32[]{:S(2)}, u32[]{:S(2)}) collective-permute-start(f32[1,32,1,128]{3,2,1,0:T(1,128)S(1)} %get-tuple-element.143), channel_id=1, source_target_pairs={{0,1},{1,2},{2,3},{3,4},{4,5},{5,6},{6,7},{7,8},{8,9},{9,10},{10,1... | collective-permute-start | bytes 49160 | tf_op jit(solution)/shard_map/ppermute | solution.py:38
  40.5 4.1 collective-permute-start.7
  46.3 2.9 collective-permute-done.6
  49.3 3.7 multiply_reduce_fusion.7
  53.0 8.5 %all-reduce.71 = (f32[]{:T(128)}, f32[]{:T(128)}) all-reduce(f32[]{:T(128)} %get-tuple-element.10, f32[]{:T(128)} %get-tuple-element.9), channel_id=1, replica_groups=mesh['gx_0'=2,'gx_1'=4,'gy_0'=4,'gy_1'=2,'gy_2'=2] {'gx_0'}, use_global_device_ids=true, to_apply=%region_1.2 | all-reduce | flops 2 | bytes 16 | tf_op jit(solution)/shard_map/psum | solution.py:52
  61.5 10.8 %all-reduce.53 = (f32[]{:T(128)}, f32[]{:T(128)}) all-reduce(f32[]{:T(128)} %get-tuple-element.69, f32[]{:T(128)} %get-tuple-element.70), channel_id=1, replica_groups=mesh['gx_0'=2,'gx_1'=4,'gy_0'=4,'gy_1'=2,'gy_2'=2] {'gx_1'}, use_global_device_ids=true, to_apply=%region_2.3 | all-reduce | flops 2 | bytes 16 | tf_op jit(solution)/shard_map/psum | solution.py:52
  72.3 9.3 %all-reduce.47 = (f32[]{:T(128)}, f32[]{:T(128)}) all-reduce(f32[]{:T(128)} %get-tuple-element.33, f32[]{:T(128)} %get-tuple-element.34), channel_id=1, replica_groups=mesh['gx_0'=2,'gx_1'=4,'gy_0'=4,'gy_1'=2,'gy_2'=2] {'gy_0'}, use_global_device_ids=true, to_apply=%region_3.4 | all-reduce | flops 2 | bytes 16 | tf_op jit(solution)/shard_map/psum | solution.py:52
  81.6 6.3 %all-reduce.65 = (f32[]{:T(128)}, f32[]{:T(128)}) all-reduce(f32[]{:T(128)} %get-tuple-element.21, f32[]{:T(128)} %get-tuple-element.22), channel_id=1, replica_groups=mesh['gx_0'=2,'gx_1'=4,'gy_0'=4,'gy_1'=2,'gy_2'=2] {'gy_1'}, use_global_device_ids=true, to_apply=%region_4.5 | all-reduce | flops 2 | bytes 16 | tf_op jit(solution)/shard_map/psum | solution.py:52
  87.9 10.8 %all-reduce.59 = (f32[]{:T(128)}, f32[]{:T(128)}) all-reduce(f32[]{:T(128)} %get-tuple-element.57, f32[]{:T(128)} %get-tuple-element.58), channel_id=1, replica_groups=mesh['gx_0'=2,'gx_1'=4,'gy_0'=4,'gy_1'=2,'gy_2'=2] {'gy_2'}, use_global_device_ids=true, to_apply=%region_5.6 | all-reduce | flops 2 | bytes 16 | tf_op jit(solution)/shard_map/psum | solution.py:52
  105.2 4.8 collective-permute-start.13
  113.0 2.9 collective-permute-done.10
  116.0 2.9 fusion
  118.9 5.1 %all-reduce.70 = (f32[]{:T(128)}, f32[]{:T(128)}) all-reduce(f32[]{:T(128)} %get-tuple-element.83, f32[]{:T(128)} %fusion), channel_id=1, replica_groups=mesh['gx_0'=2,'gx_1'=4,'gy_0'=4,'gy_1'=2,'gy_2'=2] {'gx_0'}, use_global_device_ids=true, to_apply=%region_13.14 | all-reduce | flops 2 | bytes 16 | tf_op jit(solution)/shard_map/psum | solution.py:52
  124.0 10.8 %all-reduce.52 = (f32[]{:T(128)}, f32[]{:T(128)}) all-reduce(f32[]{:T(128)} %get-tuple-element.67, f32[]{:T(128)} %get-tuple-element.68), channel_id=1, replica_groups=mesh['gx_0'=2,'gx_1'=4,'gy_0'=4,'gy_1'=2,'gy_2'=2] {'gx_1'}, use_global_device_ids=true, to_apply=%region_14.15 | all-reduce | flops 2 | bytes 16 | tf_op jit(solution)/shard_map/psum | solution.py:52
  134.8 6.6 %all-reduce.46 = (f32[]{:T(128)}, f32[]{:T(128)}) all-reduce(f32[]{:T(128)} %get-tuple-element.31, f32[]{:T(128)} %get-tuple-element.32), channel_id=1, replica_groups=mesh['gx_0'=2,'gx_1'=4,'gy_0'=4,'gy_1'=2,'gy_2'=2] {'gy_0'}, use_global_device_ids=true, to_apply=%region_15.16 | all-reduce | flops 2 | bytes 16 | tf_op jit(solution)/shard_map/psum | solution.py:52
  141.4 6.0 %all-reduce.64 = (f32[]{:T(128)}, f32[]{:T(128)}) all-reduce(f32[]{:T(128)} %get-tuple-element.19, f32[]{:T(128)} %get-tuple-element.20), channel_id=1, replica_groups=mesh['gx_0'=2,'gx_1'=4,'gy_0'=4,'gy_1'=2,'gy_2'=2] {'gy_1'}, use_global_device_ids=true, to_apply=%region_16.17 | all-reduce | flops 2 | bytes 16 | tf_op jit(solution)/shard_map/psum | solution.py:52
  147.4 8.7 %all-reduce.58 = (f32[]{:T(128)}, f32[]{:T(128)}) all-reduce(f32[]{:T(128)} %get-tuple-element.55, f32[]{:T(128)} %get-tuple-element.56), channel_id=1, replica_groups=mesh['gx_0'=2,'gx_1'=4,'gy_0'=4,'gy_1'=2,'gy_2'=2] {'gy_2'}, use_global_device_ids=true, to_apply=%region_17.18 | all-reduce | flops 2 | bytes 16 | tf_op jit(solution)/shard_map/psum | solution.py:52
  166.0 4.8 collective-permute-start.17
  179.4 5.2 %fusion.20 = f32[32,64,128]{2,1,0:T(8,128)S(1)} fusion(f32[2,32,64,127]{3,2,1,0:T(8,128)} %slice_maximum_fusion.2, f32[2,32,64,128]{3,2,1,0:T(8,128)S(1)} %select_maximum_fusion.10, f32[2,34,65,128]{3,2,1,0:T(8,128)} %get-tuple-element.97, f32[2,34,65,128]{3,2,1,0:T(8,128)S(1)} %get-tuple-element.96, f32[2,1,64,128]{3,2,1,0:T(8,128)S(1)} %collective-permute-done.15, ...), kind=kLoop, calls=%fused_computation.51 | loop fusion | flops 16515072 | bytes 26574848 | tf_op jit(solution)/shard_map/add | solution.py:97
  186.5 5.1 %collective-permute-start.21 = (f32[1,32,1,128]{3,2,1,0:T(1,128)S(1)}, f32[1,32,1,128]{3,2,1,0:T(1,128)S(1)}, u32[]{:S(2)}, u32[]{:S(2)}) collective-permute-start(f32[1,32,1,128]{3,2,1,0:T(1,128)S(1)} %get-tuple-element.131), channel_id=1, source_target_pairs={{0,1},{1,2},{2,3},{3,4},{4,5},{5,6},{6,7},{7,8},{8,9},{9,10},{10,1... | collective-permute-start | bytes 49160 | tf_op jit(solution)/shard_map/ppermute | solution.py:38
  191.7 4.2 collective-permute-start.19
  197.6 2.9 collective-permute-done.18
  200.5 3.8 multiply_reduce_fusion.4
  204.3 7.2 %all-reduce.69 = (f32[]{:T(128)}, f32[]{:T(128)}) all-reduce(f32[]{:T(128)} %get-tuple-element.8, f32[]{:T(128)} %get-tuple-element.7), channel_id=1, replica_groups=mesh['gx_0'=2,'gx_1'=4,'gy_0'=4,'gy_1'=2,'gy_2'=2] {'gx_0'}, use_global_device_ids=true, to_apply=%region_25.26 | all-reduce | flops 2 | bytes 16 | tf_op jit(solution)/shard_map/psum | solution.py:52
  211.5 10.8 %all-reduce.51 = (f32[]{:T(128)}, f32[]{:T(128)}) all-reduce(f32[]{:T(128)} %get-tuple-element.65, f32[]{:T(128)} %get-tuple-element.66), channel_id=1, replica_groups=mesh['gx_0'=2,'gx_1'=4,'gy_0'=4,'gy_1'=2,'gy_2'=2] {'gx_1'}, use_global_device_ids=true, to_apply=%region_26.27 | all-reduce | flops 2 | bytes 16 | tf_op jit(solution)/shard_map/psum | solution.py:52
  222.3 7.5 %all-reduce.45 = (f32[]{:T(128)}, f32[]{:T(128)}) all-reduce(f32[]{:T(128)} %get-tuple-element.29, f32[]{:T(128)} %get-tuple-element.30), channel_id=1, replica_groups=mesh['gx_0'=2,'gx_1'=4,'gy_0'=4,'gy_1'=2,'gy_2'=2] {'gy_0'}, use_global_device_ids=true, to_apply=%region_27.28 | all-reduce | flops 2 | bytes 16 | tf_op jit(solution)/shard_map/psum | solution.py:52
  229.9 8.0 %all-reduce.63 = (f32[]{:T(128)}, f32[]{:T(128)}) all-reduce(f32[]{:T(128)} %get-tuple-element.17, f32[]{:T(128)} %get-tuple-element.18), channel_id=1, replica_groups=mesh['gx_0'=2,'gx_1'=4,'gy_0'=4,'gy_1'=2,'gy_2'=2] {'gy_1'}, use_global_device_ids=true, to_apply=%region_28.29 | all-reduce | flops 2 | bytes 16 | tf_op jit(solution)/shard_map/psum | solution.py:52
  237.9 8.6 %all-reduce.57 = (f32[]{:T(128)}, f32[]{:T(128)}) all-reduce(f32[]{:T(128)} %get-tuple-element.53, f32[]{:T(128)} %get-tuple-element.54), channel_id=1, replica_groups=mesh['gx_0'=2,'gx_1'=4,'gy_0'=4,'gy_1'=2,'gy_2'=2] {'gy_2'}, use_global_device_ids=true, to_apply=%region_29.30 | all-reduce | flops 2 | bytes 16 | tf_op jit(solution)/shard_map/psum | solution.py:52
  252.9 4.8 collective-permute-start.25
  260.7 2.9 collective-permute-done.22
  263.7 2.9 fusion.1
  266.5 5.1 %all-reduce.68 = (f32[]{:T(128)}, f32[]{:T(128)}) all-reduce(f32[]{:T(128)} %get-tuple-element.78, f32[]{:T(128)} %fusion.1), channel_id=1, replica_groups=mesh['gx_0'=2,'gx_1'=4,'gy_0'=4,'gy_1'=2,'gy_2'=2] {'gx_0'}, use_global_device_ids=true, to_apply=%region_37.38 | all-reduce | flops 2 | bytes 16 | tf_op jit(solution)/shard_map/psum | solution.py:52
  271.7 10.8 %all-reduce.50 = (f32[]{:T(128)}, f32[]{:T(128)}) all-reduce(f32[]{:T(128)} %get-tuple-element.63, f32[]{:T(128)} %get-tuple-element.64), channel_id=1, replica_groups=mesh['gx_0'=2,'gx_1'=4,'gy_0'=4,'gy_1'=2,'gy_2'=2] {'gx_1'}, use_global_device_ids=true, to_apply=%region_38.39 | all-reduce | flops 2 | bytes 16 | tf_op jit(solution)/shard_map/psum | solution.py:52
  282.5 7.9 %all-reduce.44 = (f32[]{:T(128)}, f32[]{:T(128)}) all-reduce(f32[]{:T(128)} %get-tuple-element.27, f32[]{:T(128)} %get-tuple-element.28), channel_id=1, replica_groups=mesh['gx_0'=2,'gx_1'=4,'gy_0'=4,'gy_1'=2,'gy_2'=2] {'gy_0'}, use_global_device_ids=true, to_apply=%region_39.40 | all-reduce | flops 2 | bytes 16 | tf_op jit(solution)/shard_map/psum | solution.py:52
  290.4 6.0 %all-reduce.62 = (f32[]{:T(128)}, f32[]{:T(128)}) all-reduce(f32[]{:T(128)} %get-tuple-element.15, f32[]{:T(128)} %get-tuple-element.16), channel_id=1, replica_groups=mesh['gx_0'=2,'gx_1'=4,'gy_0'=4,'gy_1'=2,'gy_2'=2] {'gy_1'}, use_global_device_ids=true, to_apply=%region_40.41 | all-reduce | flops 2 | bytes 16 | tf_op jit(solution)/shard_map/psum | solution.py:52
  296.4 8.4 %all-reduce.56 = (f32[]{:T(128)}, f32[]{:T(128)}) all-reduce(f32[]{:T(128)} %get-tuple-element.51, f32[]{:T(128)} %get-tuple-element.52), channel_id=1, replica_groups=mesh['gx_0'=2,'gx_1'=4,'gy_0'=4,'gy_1'=2,'gy_2'=2] {'gy_2'}, use_global_device_ids=true, to_apply=%region_41.42 | all-reduce | flops 2 | bytes 16 | tf_op jit(solution)/shard_map/psum | solution.py:52
  316.6 4.8 collective-permute-start.29
  330.0 5.6 %fusion.31 = f32[32,64,128]{2,1,0:T(8,128)S(1)} fusion(f32[2,32,64,127]{3,2,1,0:T(8,128)} %slice_maximum_fusion.1, f32[2,32,64,128]{3,2,1,0:T(8,128)} %select_maximum_fusion.9, f32[2,34,65,128]{3,2,1,0:T(8,128)} %get-tuple-element.95, f32[2,34,65,128]{3,2,1,0:T(8,128)S(1)} %get-tuple-element.94, f32[2,1,64,128]{3,2,1,0:T(8,128)S(1)} %collective-permute-done.27, ...), kind=kLoop, calls=%fused_computation.62 | loop fusion | flops 17563648 | bytes 27623424 | tf_op jit(solution)/shard_map/add | solution.py:97
  337.6 5.1 %collective-permute-start.33 = (f32[1,32,1,128]{3,2,1,0:T(1,128)S(1)}, f32[1,32,1,128]{3,2,1,0:T(1,128)S(1)}, u32[]{:S(2)}, u32[]{:S(2)}) collective-permute-start(f32[1,32,1,128]{3,2,1,0:T(1,128)S(1)} %get-tuple-element.119), channel_id=1, source_target_pairs={{0,1},{1,2},{2,3},{3,4},{4,5},{5,6},{6,7},{7,8},{8,9},{9,10},{10,1... | collective-permute-start | bytes 49160 | tf_op jit(solution)/shard_map/ppermute | solution.py:38
  342.8 4.2 collective-permute-start.31
  348.7 2.9 collective-permute-done.30
  351.6 3.7 multiply_reduce_fusion.1
  355.4 7.3 %all-reduce.67 = (f32[]{:T(128)}, f32[]{:T(128)}) all-reduce(f32[]{:T(128)} %get-tuple-element.6, f32[]{:T(128)} %get-tuple-element.5), channel_id=1, replica_groups=mesh['gx_0'=2,'gx_1'=4,'gy_0'=4,'gy_1'=2,'gy_2'=2] {'gx_0'}, use_global_device_ids=true, to_apply=%region_49.50 | all-reduce | flops 2 | bytes 16 | tf_op jit(solution)/shard_map/psum | solution.py:52
  362.6 10.7 %all-reduce.49 = (f32[]{:T(128)}, f32[]{:T(128)}) all-reduce(f32[]{:T(128)} %get-tuple-element.61, f32[]{:T(128)} %get-tuple-element.62), channel_id=1, replica_groups=mesh['gx_0'=2,'gx_1'=4,'gy_0'=4,'gy_1'=2,'gy_2'=2] {'gx_1'}, use_global_device_ids=true, to_apply=%region_50.51 | all-reduce | flops 2 | bytes 16 | tf_op jit(solution)/shard_map/psum | solution.py:52
  373.4 7.0 %all-reduce.43 = (f32[]{:T(128)}, f32[]{:T(128)}) all-reduce(f32[]{:T(128)} %get-tuple-element.25, f32[]{:T(128)} %get-tuple-element.26), channel_id=1, replica_groups=mesh['gx_0'=2,'gx_1'=4,'gy_0'=4,'gy_1'=2,'gy_2'=2] {'gy_0'}, use_global_device_ids=true, to_apply=%region_51.52 | all-reduce | flops 2 | bytes 16 | tf_op jit(solution)/shard_map/psum | solution.py:52
  380.4 7.6 %all-reduce.61 = (f32[]{:T(128)}, f32[]{:T(128)}) all-reduce(f32[]{:T(128)} %get-tuple-element.13, f32[]{:T(128)} %get-tuple-element.14), channel_id=1, replica_groups=mesh['gx_0'=2,'gx_1'=4,'gy_0'=4,'gy_1'=2,'gy_2'=2] {'gy_1'}, use_global_device_ids=true, to_apply=%region_52.53 | all-reduce | flops 2 | bytes 16 | tf_op jit(solution)/shard_map/psum | solution.py:52
  387.9 10.2 %all-reduce.55 = (f32[]{:T(128)}, f32[]{:T(128)}) all-reduce(f32[]{:T(128)} %get-tuple-element.49, f32[]{:T(128)} %get-tuple-element.50), channel_id=1, replica_groups=mesh['gx_0'=2,'gx_1'=4,'gy_0'=4,'gy_1'=2,'gy_2'=2] {'gy_2'}, use_global_device_ids=true, to_apply=%region_53.54 | all-reduce | flops 2 | bytes 16 | tf_op jit(solution)/shard_map/psum | solution.py:52
  404.5 4.8 collective-permute-start.37
  412.4 2.9 collective-permute-done.34
  415.3 2.8 fusion.2
  418.2 5.1 %all-reduce.66 = (f32[]{:T(128)}, f32[]{:T(128)}) all-reduce(f32[]{:T(128)} %get-tuple-element.73, f32[]{:T(128)} %fusion.2), channel_id=1, replica_groups=mesh['gx_0'=2,'gx_1'=4,'gy_0'=4,'gy_1'=2,'gy_2'=2] {'gx_0'}, use_global_device_ids=true, to_apply=%region_61.62 | all-reduce | flops 2 | bytes 16 | tf_op jit(solution)/shard_map/psum | solution.py:52
  423.2 10.8 %all-reduce.48 = (f32[]{:T(128)}, f32[]{:T(128)}) all-reduce(f32[]{:T(128)} %get-tuple-element.59, f32[]{:T(128)} %get-tuple-element.60), channel_id=1, replica_groups=mesh['gx_0'=2,'gx_1'=4,'gy_0'=4,'gy_1'=2,'gy_2'=2] {'gx_1'}, use_global_device_ids=true, to_apply=%region_62.63 | all-reduce | flops 2 | bytes 16 | tf_op jit(solution)/shard_map/psum | solution.py:52
  434.0 6.6 %all-reduce.42 = (f32[]{:T(128)}, f32[]{:T(128)}) all-reduce(f32[]{:T(128)} %get-tuple-element.23, f32[]{:T(128)} %get-tuple-element.24), channel_id=1, replica_groups=mesh['gx_0'=2,'gx_1'=4,'gy_0'=4,'gy_1'=2,'gy_2'=2] {'gy_0'}, use_global_device_ids=true, to_apply=%region_63.64 | all-reduce | flops 2 | bytes 16 | tf_op jit(solution)/shard_map/psum | solution.py:52
  440.6 5.9 %all-reduce.60 = (f32[]{:T(128)}, f32[]{:T(128)}) all-reduce(f32[]{:T(128)} %get-tuple-element.11, f32[]{:T(128)} %get-tuple-element.12), channel_id=1, replica_groups=mesh['gx_0'=2,'gx_1'=4,'gy_0'=4,'gy_1'=2,'gy_2'=2] {'gy_1'}, use_global_device_ids=true, to_apply=%region_64.65 | all-reduce | flops 2 | bytes 16 | tf_op jit(solution)/shard_map/psum | solution.py:52
  446.5 8.6 %all-reduce.54 = (f32[]{:T(128)}, f32[]{:T(128)}) all-reduce(f32[]{:T(128)} %get-tuple-element.47, f32[]{:T(128)} %get-tuple-element.48), channel_id=1, replica_groups=mesh['gx_0'=2,'gx_1'=4,'gy_0'=4,'gy_1'=2,'gy_2'=2] {'gy_2'}, use_global_device_ids=true, to_apply=%region_65.66 | all-reduce | flops 2 | bytes 16 | tf_op jit(solution)/shard_map/psum | solution.py:52
  459.5 3.3 fusion.325
  466.4 4.8 collective-permute-start.41
  477.5 2.8 select_maximum_fusion.1
  480.4 6.8 %fusion.46 = f32[32,64,128]{2,1,0:T(8,128)} fusion(f32[32,64,128]{2,1,0:T(8,128)S(1)} %copy-done.32, f32[32,64,128]{2,1,0:T(8,128)S(1)} %copy-done.40, f32[32,64,128]{2,1,0:T(8,128)S(1)} %get-tuple-element.72, f32[32,64,128]{2,1,0:T(8,128)S(1)} %copy-done.4, f32[2,32,64,127]{3,2,1,0:T(8,128)} %slice_maximum_fusion, ...), kind=kLoop, calls=%fused_computation.77 | loop fusion | flops 19398656 | bytes 28672000 | tf_op jit(solution)/shard_map/add | solution.py:164
  (237 shorter events, 87.7 us)
Async XLA Ops:
  0.0 14.9 %copy-start = (f32[3,32,64,128]{3,2,1,0:T(8,128)S(1)}, f32[3,32,64,128]{3,2,1,0:T(8,128)}, u32[]{:S(2)}) copy-start(f32[3,32,64,128]{3,2,1,0:T(8,128)} %param.6) | copy-start | bytes 9437188
  0.0 14.9 %copy-start.57 = (s32[3,32,64]{2,1,0:T(8,128)S(1)}, s32[3,32,64]{2,1,0:T(8,128)}, u32[]{:S(2)}) copy-start(s32[3,32,64]{2,1,0:T(8,128)} %param.7) | copy-start | bytes 73732
  1.5 26.7 %collective-permute-start.3 = (f32[2,32,1,128]{3,2,1,0:T(1,128)S(1)}, f32[2,32,1,128]{3,2,1,0:T(1,128)S(1)}, u32[]{:S(2)}, u32[]{:S(2)}) collective-permute-start(f32[2,32,1,128]{3,2,1,0:T(1,128)S(1)} %get-tuple-element.148), channel_id=1, source_target_pairs={{1,0},{2,1},{3,2},{4,3},{5,4},{6,5},{7,6},{8,7},{9,8},{10,9},{11,1... | collective-permute-start | bytes 98312 | tf_op jit(solution)/shard_map/ppermute | solution.py:39
  4.8 23.4 %collective-permute-start.5 = (f32[2,32,1,128]{3,2,1,0:T(1,128)S(1)}, f32[2,32,1,128]{3,2,1,0:T(1,128)S(1)}, u32[]{:S(2)}, u32[]{:S(2)}) collective-permute-start(f32[2,32,1,128]{3,2,1,0:T(1,128)S(1)} %get-tuple-element.149), channel_id=1, source_target_pairs={{0,1},{1,2},{2,3},{3,4},{4,5},{5,6},{6,7},{7,8},{8,9},{9,10},{10,1... | collective-permute-start | bytes 98312 | tf_op jit(solution)/shard_map/ppermute | solution.py:38
  10.3 17.9 %collective-permute-start.2 = (f32[2,1,64,128]{3,2,1,0:T(8,128)S(1)}, f32[2,1,64,128]{3,2,1,0:T(8,128)S(1)}, u32[]{:S(2)}, u32[]{:S(2)}) collective-permute-start(f32[2,1,64,128]{3,2,1,0:T(8,128)S(1)} %get-tuple-element.150), channel_id=1, source_target_pairs={{0,16},{16,32},{32,48},{48,64},{64,80},{80,96},{96,112},{1,17},{17... | collective-permute-start | bytes 196616 | tf_op jit(solution)/shard_map/ppermute | solution.py:38
  13.6 14.7 %collective-permute-start = (f32[2,1,64,128]{3,2,1,0:T(8,128)S(1)}, f32[2,1,64,128]{3,2,1,0:T(8,128)S(1)}, u32[]{:S(2)}, u32[]{:S(2)}) collective-permute-start(f32[2,1,64,128]{3,2,1,0:T(8,128)S(1)} %get-tuple-element.151), channel_id=1, source_target_pairs={{16,0},{32,16},{48,32},{64,48},{80,64},{96,80},{112,96},{17,1},{33... | collective-permute-start | bytes 196616 | tf_op jit(solution)/shard_map/ppermute | solution.py:39
  17.4 4.6 collective-permute-start.4
  21.5 27.8 %copy-start.5 = (f32[32,64,128]{2,1,0:T(8,128)}, f32[32,64,128]{2,1,0:T(8,128)S(1)}, u32[]{:S(2)}) copy-start(f32[32,64,128]{2,1,0:T(8,128)S(1)} %get-tuple-element.88) | copy-start | bytes 3145732
  21.5 27.8 %copy-start.12 = (f32[32,64,128]{2,1,0:T(8,128)}, f32[32,64,128]{2,1,0:T(8,128)S(1)}, u32[]{:S(2)}) copy-start(f32[32,64,128]{2,1,0:T(8,128)S(1)} %get-tuple-element.89) | copy-start | bytes 3145732
  21.7 27.5 %copy-start.19 = (f32[31,64,128]{2,1,0:T(8,128)}, f32[31,64,128]{2,1,0:T(8,128)S(1)}, u32[]{:S(2)}) copy-start(f32[31,64,128]{2,1,0:T(8,128)S(1)} %get-tuple-element.157) | copy-start | bytes 3047428
  22.0 6.2 %collective-permute-start.1 = (f32[2,1,64,128]{3,2,1,0:T(8,128)S(1)}, f32[2,1,64,128]{3,2,1,0:T(8,128)S(1)}, u32[]{:S(2)}, u32[]{:S(2)}) collective-permute-start(f32[2,1,64,128]{3,2,1,0:T(8,128)S(1)} %pad_maximum_fusion.64), channel_id=1, source_target_pairs={{0,16},{16,32},{32,48},{48,64},{64,80},{80,96},{96,112},{1,17},{17... | collective-permute-start | bytes 196616 | tf_op jit(solution)/shard_map/ppermute | solution.py:59
  33.2 19.8 %copy-start.33 = (f32[32,64,128]{2,1,0:T(8,128)}, f32[32,64,128]{2,1,0:T(8,128)S(1)}, u32[]{:S(2)}) copy-start(f32[32,64,128]{2,1,0:T(8,128)S(1)} %get-tuple-element.86) | copy-start | bytes 3145732
  33.3 13.0 %collective-permute-start.8 = (f32[1,32,1,128]{3,2,1,0:T(1,128)S(1)}, f32[1,32,1,128]{3,2,1,0:T(1,128)S(1)}, u32[]{:S(2)}, u32[]{:S(2)}) collective-permute-start(f32[1,32,1,128]{3,2,1,0:T(1,128)S(1)} %get-tuple-element.142), channel_id=1, source_target_pairs={{1,0},{2,1},{3,2},{4,3},{5,4},{6,5},{7,6},{8,7},{9,8},{10,9},{11,1... | collective-permute-start | bytes 49160 | tf_op jit(solution)/shard_map/ppermute | solution.py:39
  35.4 10.9 %collective-permute-start.9 = (f32[1,32,1,128]{3,2,1,0:T(1,128)S(1)}, f32[1,32,1,128]{3,2,1,0:T(1,128)S(1)}, u32[]{:S(2)}, u32[]{:S(2)}) collective-permute-start(f32[1,32,1,128]{3,2,1,0:T(1,128)S(1)} %get-tuple-element.143), channel_id=1, source_target_pairs={{0,1},{1,2},{2,3},{3,4},{4,5},{5,6},{6,7},{7,8},{8,9},{9,10},{10,1... | collective-permute-start | bytes 49160 | tf_op jit(solution)/shard_map/ppermute | solution.py:38
  40.5 5.8 %collective-permute-start.7 = (f32[1,1,64,128]{3,2,1,0:T(8,128)S(1)}, f32[1,1,64,128]{3,2,1,0:T(8,128)S(1)}, u32[]{:S(2)}, u32[]{:S(2)}) collective-permute-start(f32[1,1,64,128]{3,2,1,0:T(8,128)S(1)} %get-tuple-element.144), channel_id=1, source_target_pairs={{0,16},{16,32},{32,48},{48,64},{64,80},{80,96},{96,112},{1,17},{17... | collective-permute-start | bytes 98312 | tf_op jit(solution)/shard_map/ppermute | solution.py:38
  44.6 4.7 collective-permute-start.6
  102.6 16.2 %copy-start.36 = (f32[32,64,128]{2,1,0:T(8,128)}, f32[32,64,128]{2,1,0:T(8,128)S(1)}, u32[]{:S(2)}) copy-start(f32[32,64,128]{2,1,0:T(8,128)S(1)} %get-tuple-element.84) | copy-start | bytes 3145732
  102.6 13.4 %copy-start.6 = (f32[32,64,128]{2,1,0:T(8,128)S(1)}, f32[32,64,128]{2,1,0:T(8,128)}, u32[]{:S(2)}) copy-start(f32[32,64,128]{2,1,0:T(8,128)} %copy-done.5) | copy-start | bytes 3145732
  102.6 13.4 %copy-start.13 = (f32[32,64,128]{2,1,0:T(8,128)S(1)}, f32[32,64,128]{2,1,0:T(8,128)}, u32[]{:S(2)}) copy-start(f32[32,64,128]{2,1,0:T(8,128)} %copy-done.12) | copy-start | bytes 3145732
  102.6 13.4 %copy-start.20 = (f32[31,64,128]{2,1,0:T(8,128)S(1)}, f32[31,64,128]{2,1,0:T(8,128)}, u32[]{:S(2)}) copy-start(f32[31,64,128]{2,1,0:T(8,128)} %copy-done.19) | copy-start | bytes 3047428
  102.7 10.3 %collective-permute-start.12 = (f32[1,32,1,128]{3,2,1,0:T(1,128)S(1)}, f32[1,32,1,128]{3,2,1,0:T(1,128)S(1)}, u32[]{:S(2)}, u32[]{:S(2)}) collective-permute-start(f32[1,32,1,128]{3,2,1,0:T(1,128)S(1)} %get-tuple-element.138), channel_id=1, source_target_pairs={{1,0},{2,1},{3,2},{4,3},{5,4},{6,5},{7,6},{8,7},{9,8},{10,9},{11,1... | collective-permute-start | bytes 49160 | tf_op jit(solution)/shard_map/ppermute | solution.py:39
  105.2 7.8 %collective-permute-start.13 = (f32[1,32,1,128]{3,2,1,0:T(1,128)S(1)}, f32[1,32,1,128]{3,2,1,0:T(1,128)S(1)}, u32[]{:S(2)}, u32[]{:S(2)}) collective-permute-start(f32[1,32,1,128]{3,2,1,0:T(1,128)S(1)} %get-tuple-element.139), channel_id=1, source_target_pairs={{0,1},{1,2},{2,3},{3,4},{4,5},{5,6},{6,7},{7,8},{8,9},{9,10},{10,1... | collective-permute-start | bytes 49160 | tf_op jit(solution)/shard_map/ppermute | solution.py:38
  110.0 3.0 collective-permute-start.11
  111.3 4.7 collective-permute-start.10
  162.8 16.5 %copy-start.30 = (f32[32,64,128]{2,1,0:T(8,128)}, f32[32,64,128]{2,1,0:T(8,128)S(1)}, u32[]{:S(2)}) copy-start(f32[32,64,128]{2,1,0:T(8,128)S(1)} %get-tuple-element.82) | copy-start | bytes 3145732
  163.8 11.8 %collective-permute-start.16 = (f32[2,32,1,128]{3,2,1,0:T(1,128)S(1)}, f32[2,32,1,128]{3,2,1,0:T(1,128)S(1)}, u32[]{:S(2)}, u32[]{:S(2)}) collective-permute-start(f32[2,32,1,128]{3,2,1,0:T(1,128)S(1)} %get-tuple-element.106), channel_id=1, source_target_pairs={{1,0},{2,1},{3,2},{4,3},{5,4},{6,5},{7,6},{8,7},{9,8},{10,9},{11,1... | collective-permute-start | bytes 98312 | tf_op jit(solution)/shard_map/ppermute | solution.py:39
  166.0 9.6 %collective-permute-start.17 = (f32[2,32,1,128]{3,2,1,0:T(1,128)S(1)}, f32[2,32,1,128]{3,2,1,0:T(1,128)S(1)}, u32[]{:S(2)}, u32[]{:S(2)}) collective-permute-start(f32[2,32,1,128]{3,2,1,0:T(1,128)S(1)} %get-tuple-element.107), channel_id=1, source_target_pairs={{0,1},{1,2},{2,3},{3,4},{4,5},{5,6},{6,7},{7,8},{8,9},{9,10},{10,1... | collective-permute-start | bytes 98312 | tf_op jit(solution)/shard_map/ppermute | solution.py:38
  170.8 4.8 collective-permute-start.15
  172.2 5.0 %collective-permute-start.14 = (f32[2,1,64,128]{3,2,1,0:T(8,128)S(1)}, f32[2,1,64,128]{3,2,1,0:T(8,128)S(1)}, u32[]{:S(2)}, u32[]{:S(2)}) collective-permute-start(f32[2,1,64,128]{3,2,1,0:T(8,128)S(1)} %get-tuple-element.109), channel_id=1, source_target_pairs={{16,0},{32,16},{48,32},{64,48},{80,64},{96,80},{112,96},{17,1},{33... | collective-permute-start | bytes 196616 | tf_op jit(solution)/shard_map/ppermute | solution.py:39
  184.5 19.8 %copy-start.34 = (f32[32,64,128]{2,1,0:T(8,128)}, f32[32,64,128]{2,1,0:T(8,128)S(1)}, u32[]{:S(2)}) copy-start(f32[32,64,128]{2,1,0:T(8,128)S(1)} %fusion.20) | copy-start | bytes 3145732
  184.6 13.0 %collective-permute-start.20 = (f32[1,32,1,128]{3,2,1,0:T(1,128)S(1)}, f32[1,32,1,128]{3,2,1,0:T(1,128)S(1)}, u32[]{:S(2)}, u32[]{:S(2)}) collective-permute-start(f32[1,32,1,128]{3,2,1,0:T(1,128)S(1)} %get-tuple-element.130), channel_id=1, source_target_pairs={{1,0},{2,1},{3,2},{4,3},{5,4},{6,5},{7,6},{8,7},{9,8},{10,9},{11,1... | collective-permute-start | bytes 49160 | tf_op jit(solution)/shard_map/ppermute | solution.py:39
  186.5 11.0 %collective-permute-start.21 = (f32[1,32,1,128]{3,2,1,0:T(1,128)S(1)}, f32[1,32,1,128]{3,2,1,0:T(1,128)S(1)}, u32[]{:S(2)}, u32[]{:S(2)}) collective-permute-start(f32[1,32,1,128]{3,2,1,0:T(1,128)S(1)} %get-tuple-element.131), channel_id=1, source_target_pairs={{0,1},{1,2},{2,3},{3,4},{4,5},{5,6},{6,7},{7,8},{8,9},{9,10},{10,1... | collective-permute-start | bytes 49160 | tf_op jit(solution)/shard_map/ppermute | solution.py:38
  191.7 5.9 %collective-permute-start.19 = (f32[1,1,64,128]{3,2,1,0:T(8,128)S(1)}, f32[1,1,64,128]{3,2,1,0:T(8,128)S(1)}, u32[]{:S(2)}, u32[]{:S(2)}) collective-permute-start(f32[1,1,64,128]{3,2,1,0:T(8,128)S(1)} %get-tuple-element.132), channel_id=1, source_target_pairs={{0,16},{16,32},{32,48},{48,64},{64,80},{80,96},{96,112},{1,17},{17... | collective-permute-start | bytes 98312 | tf_op jit(solution)/shard_map/ppermute | solution.py:38
  195.9 4.7 collective-permute-start.18
  250.3 16.2 %copy-start.37 = (f32[32,64,128]{2,1,0:T(8,128)}, f32[32,64,128]{2,1,0:T(8,128)S(1)}, u32[]{:S(2)}) copy-start(f32[32,64,128]{2,1,0:T(8,128)S(1)} %get-tuple-element.79) | copy-start | bytes 3145732
  250.3 13.4 %copy-start.8 = (f32[32,64,128]{2,1,0:T(8,128)S(1)}, f32[32,64,128]{2,1,0:T(8,128)}, u32[]{:S(2)}) copy-start(f32[32,64,128]{2,1,0:T(8,128)} %copy-done.5) | copy-start | bytes 3145732
  250.3 13.4 %copy-start.15 = (f32[32,64,128]{2,1,0:T(8,128)S(1)}, f32[32,64,128]{2,1,0:T(8,128)}, u32[]{:S(2)}) copy-start(f32[32,64,128]{2,1,0:T(8,128)} %copy-done.12) | copy-start | bytes 3145732
  250.3 13.4 %copy-start.22 = (f32[31,64,128]{2,1,0:T(8,128)S(1)}, f32[31,64,128]{2,1,0:T(8,128)}, u32[]{:S(2)}) copy-start(f32[31,64,128]{2,1,0:T(8,128)} %copy-done.19) | copy-start | bytes 3047428
  250.4 10.3 %collective-permute-start.24 = (f32[1,32,1,128]{3,2,1,0:T(1,128)S(1)}, f32[1,32,1,128]{3,2,1,0:T(1,128)S(1)}, u32[]{:S(2)}, u32[]{:S(2)}) collective-permute-start(f32[1,32,1,128]{3,2,1,0:T(1,128)S(1)} %get-tuple-element.126), channel_id=1, source_target_pairs={{1,0},{2,1},{3,2},{4,3},{5,4},{6,5},{7,6},{8,7},{9,8},{10,9},{11,1... | collective-permute-start | bytes 49160 | tf_op jit(solution)/shard_map/ppermute | solution.py:39
  252.9 7.8 %collective-permute-start.25 = (f32[1,32,1,128]{3,2,1,0:T(1,128)S(1)}, f32[1,32,1,128]{3,2,1,0:T(1,128)S(1)}, u32[]{:S(2)}, u32[]{:S(2)}) collective-permute-start(f32[1,32,1,128]{3,2,1,0:T(1,128)S(1)} %get-tuple-element.127), channel_id=1, source_target_pairs={{0,1},{1,2},{2,3},{3,4},{4,5},{5,6},{6,7},{7,8},{8,9},{9,10},{10,1... | collective-permute-start | bytes 49160 | tf_op jit(solution)/shard_map/ppermute | solution.py:38
  257.7 3.0 collective-permute-start.23
  259.0 4.7 collective-permute-start.22
  311.9 18.0 %copy-start.39 = (f32[32,64,128]{2,1,0:T(8,128)}, f32[32,64,128]{2,1,0:T(8,128)S(1)}, u32[]{:S(2)}) copy-start(f32[32,64,128]{2,1,0:T(8,128)S(1)} %get-tuple-element.77) | copy-start | bytes 3145732
  314.4 11.9 %collective-permute-start.28 = (f32[2,32,1,128]{3,2,1,0:T(1,128)S(1)}, f32[2,32,1,128]{3,2,1,0:T(1,128)S(1)}, u32[]{:S(2)}, u32[]{:S(2)}) collective-permute-start(f32[2,32,1,128]{3,2,1,0:T(1,128)S(1)} %get-tuple-element.102), channel_id=1, source_target_pairs={{1,0},{2,1},{3,2},{4,3},{5,4},{6,5},{7,6},{8,7},{9,8},{10,9},{11,1... | collective-permute-start | bytes 98312 | tf_op jit(solution)/shard_map/ppermute | solution.py:39
  316.6 9.6 %collective-permute-start.29 = (f32[2,32,1,128]{3,2,1,0:T(1,128)S(1)}, f32[2,32,1,128]{3,2,1,0:T(1,128)S(1)}, u32[]{:S(2)}, u32[]{:S(2)}) collective-permute-start(f32[2,32,1,128]{3,2,1,0:T(1,128)S(1)} %get-tuple-element.103), channel_id=1, source_target_pairs={{0,1},{1,2},{2,3},{3,4},{4,5},{5,6},{6,7},{7,8},{8,9},{9,10},{10,1... | collective-permute-start | bytes 98312 | tf_op jit(solution)/shard_map/ppermute | solution.py:38
  321.4 4.8 collective-permute-start.27
  322.7 5.0 %collective-permute-start.26 = (f32[2,1,64,128]{3,2,1,0:T(8,128)S(1)}, f32[2,1,64,128]{3,2,1,0:T(8,128)S(1)}, u32[]{:S(2)}, u32[]{:S(2)}) collective-permute-start(f32[2,1,64,128]{3,2,1,0:T(8,128)S(1)} %get-tuple-element.105), channel_id=1, source_target_pairs={{16,0},{32,16},{48,32},{64,48},{80,64},{96,80},{112,96},{17,1},{33... | collective-permute-start | bytes 196616 | tf_op jit(solution)/shard_map/ppermute | solution.py:39
  335.6 19.7 %copy-start.35 = (f32[32,64,128]{2,1,0:T(8,128)}, f32[32,64,128]{2,1,0:T(8,128)S(1)}, u32[]{:S(2)}) copy-start(f32[32,64,128]{2,1,0:T(8,128)S(1)} %fusion.31) | copy-start | bytes 3145732
  335.7 12.9 %collective-permute-start.32 = (f32[1,32,1,128]{3,2,1,0:T(1,128)S(1)}, f32[1,32,1,128]{3,2,1,0:T(1,128)S(1)}, u32[]{:S(2)}, u32[]{:S(2)}) collective-permute-start(f32[1,32,1,128]{3,2,1,0:T(1,128)S(1)} %get-tuple-element.118), channel_id=1, source_target_pairs={{1,0},{2,1},{3,2},{4,3},{5,4},{6,5},{7,6},{8,7},{9,8},{10,9},{11,1... | collective-permute-start | bytes 49160 | tf_op jit(solution)/shard_map/ppermute | solution.py:39
  337.6 11.0 %collective-permute-start.33 = (f32[1,32,1,128]{3,2,1,0:T(1,128)S(1)}, f32[1,32,1,128]{3,2,1,0:T(1,128)S(1)}, u32[]{:S(2)}, u32[]{:S(2)}) collective-permute-start(f32[1,32,1,128]{3,2,1,0:T(1,128)S(1)} %get-tuple-element.119), channel_id=1, source_target_pairs={{0,1},{1,2},{2,3},{3,4},{4,5},{5,6},{6,7},{7,8},{8,9},{9,10},{10,1... | collective-permute-start | bytes 49160 | tf_op jit(solution)/shard_map/ppermute | solution.py:38
  342.8 5.9 %collective-permute-start.31 = (f32[1,1,64,128]{3,2,1,0:T(8,128)S(1)}, f32[1,1,64,128]{3,2,1,0:T(8,128)S(1)}, u32[]{:S(2)}, u32[]{:S(2)}) collective-permute-start(f32[1,1,64,128]{3,2,1,0:T(8,128)S(1)} %get-tuple-element.120), channel_id=1, source_target_pairs={{0,16},{16,32},{32,48},{48,64},{64,80},{80,96},{96,112},{1,17},{17... | collective-permute-start | bytes 98312 | tf_op jit(solution)/shard_map/ppermute | solution.py:38
  347.0 4.7 collective-permute-start.30
  401.9 16.2 %copy-start.38 = (f32[32,64,128]{2,1,0:T(8,128)}, f32[32,64,128]{2,1,0:T(8,128)S(1)}, u32[]{:S(2)}) copy-start(f32[32,64,128]{2,1,0:T(8,128)S(1)} %get-tuple-element.74) | copy-start | bytes 3145732
  401.9 13.4 %copy-start.10 = (f32[32,64,128]{2,1,0:T(8,128)S(1)}, f32[32,64,128]{2,1,0:T(8,128)}, u32[]{:S(2)}) copy-start(f32[32,64,128]{2,1,0:T(8,128)} %copy-done.5) | copy-start | bytes 3145732
  402.0 13.4 %copy-start.17 = (f32[32,64,128]{2,1,0:T(8,128)S(1)}, f32[32,64,128]{2,1,0:T(8,128)}, u32[]{:S(2)}) copy-start(f32[32,64,128]{2,1,0:T(8,128)} %copy-done.12) | copy-start | bytes 3145732
  402.0 13.4 %copy-start.24 = (f32[31,64,128]{2,1,0:T(8,128)S(1)}, f32[31,64,128]{2,1,0:T(8,128)}, u32[]{:S(2)}) copy-start(f32[31,64,128]{2,1,0:T(8,128)} %copy-done.19) | copy-start | bytes 3047428
  402.0 10.3 %collective-permute-start.36 = (f32[1,32,1,128]{3,2,1,0:T(1,128)S(1)}, f32[1,32,1,128]{3,2,1,0:T(1,128)S(1)}, u32[]{:S(2)}, u32[]{:S(2)}) collective-permute-start(f32[1,32,1,128]{3,2,1,0:T(1,128)S(1)} %get-tuple-element.114), channel_id=1, source_target_pairs={{1,0},{2,1},{3,2},{4,3},{5,4},{6,5},{7,6},{8,7},{9,8},{10,9},{11,1... | collective-permute-start | bytes 49160 | tf_op jit(solution)/shard_map/ppermute | solution.py:39
  404.5 7.8 %collective-permute-start.37 = (f32[1,32,1,128]{3,2,1,0:T(1,128)S(1)}, f32[1,32,1,128]{3,2,1,0:T(1,128)S(1)}, u32[]{:S(2)}, u32[]{:S(2)}) collective-permute-start(f32[1,32,1,128]{3,2,1,0:T(1,128)S(1)} %get-tuple-element.115), channel_id=1, source_target_pairs={{0,1},{1,2},{2,3},{3,4},{4,5},{5,6},{6,7},{7,8},{8,9},{9,10},{10,1... | collective-permute-start | bytes 49160 | tf_op jit(solution)/shard_map/ppermute | solution.py:38
  409.3 3.0 collective-permute-start.35
  410.6 4.7 collective-permute-start.34
  464.1 11.9 %collective-permute-start.40 = (f32[2,32,1,128]{3,2,1,0:T(1,128)S(1)}, f32[2,32,1,128]{3,2,1,0:T(1,128)S(1)}, u32[]{:S(2)}, u32[]{:S(2)}) collective-permute-start(f32[2,32,1,128]{3,2,1,0:T(1,128)S(1)} %get-tuple-element.98), channel_id=1, source_target_pairs={{1,0},{2,1},{3,2},{4,3},{5,4},{6,5},{7,6},{8,7},{9,8},{10,9},{11,1... | collective-permute-start | bytes 98312 | tf_op jit(solution)/shard_map/ppermute | solution.py:39
  466.4 9.6 %collective-permute-start.41 = (f32[2,32,1,128]{3,2,1,0:T(1,128)S(1)}, f32[2,32,1,128]{3,2,1,0:T(1,128)S(1)}, u32[]{:S(2)}, u32[]{:S(2)}) collective-permute-start(f32[2,32,1,128]{3,2,1,0:T(1,128)S(1)} %get-tuple-element.99), channel_id=1, source_target_pairs={{0,1},{1,2},{2,3},{3,4},{4,5},{5,6},{6,7},{7,8},{8,9},{9,10},{10,1... | collective-permute-start | bytes 98312 | tf_op jit(solution)/shard_map/ppermute | solution.py:38
  471.2 4.8 collective-permute-start.39
  472.5 5.0 %collective-permute-start.38 = (f32[2,1,64,128]{3,2,1,0:T(8,128)S(1)}, f32[2,1,64,128]{3,2,1,0:T(8,128)S(1)}, u32[]{:S(2)}, u32[]{:S(2)}) collective-permute-start(f32[2,1,64,128]{3,2,1,0:T(8,128)S(1)} %get-tuple-element.101), channel_id=1, source_target_pairs={{16,0},{32,16},{48,32},{64,48},{80,64},{96,80},{112,96},{17,1},{33... | collective-permute-start | bytes 196616 | tf_op jit(solution)/shard_map/ppermute | solution.py:39
  (36 other events, 161.9 us)
where the time goes:
time: 493 us; the launch traced here: 487 us
  blocking collectives  243 us (49%)
  starting transfers between devices  117 us (24%)
  other arithmetic  80.7 us (16%)
  waiting for transfers between devices  24.1 us (5%)
  between operations  18.6 us (4%)
    psum x30, blocking collectives, by_axis(): array = lax.psum(array, axis)  243 us
    ppermute x20, starting transfers between devices, padded(): lax.ppermute(last, axis, up)  73.2 us
    ppermute x20, starting transfers between devices, padded(): lax.ppermute(leading, axis, [(b, a) for a, b in up])  37.1 us
    ppermute x20, waiting for transfers between devices, padded(): lax.ppermute(leading, axis, [(b, a) for a, b in up])  22.2 us
    another operation x15, other arithmetic, local(): source = operate(jnp.stack([advected, diffused]))  21.1 us
    reduce_sum x6, other arithmetic, paired_products(): jnp.sum(residual * image)  19.8 us
    add x3, other arithmetic, apply_halo(): total = total + jnp.where(velocity_low[dimension] > 0, 0.0, moved_low)  14.6 us
  transfers between devices with their start and end apart: 42, of which 10 were waited for; matrix products, arithmetic and copies ran while one was open for 3% of the time, Pallas kernels for 0%

commit v1 on v0

v1 whole, which is shorter than its diff:
```python
import functools

import jax
import jax.numpy as jnp
from jax import lax
from jax.experimental import pallas as pl
from jax.experimental.pallas import tpu as pltpu
from jax.sharding import PartitionSpec as P

MESH = pl.DeviceIdType.MESH
F32 = jnp.float32

BX, BY, BZ = 32, 64, 128
OX, OY = 2, 16
EX, EY = BX + 2 * OX, BY + 2 * OY
TOP, BOT = OY, OY + BY
EXT = (EX, EY, BZ)
PARTS = {"zl": 2, "y": 4, "x": 4, "zh": 2, "c": 2}


def offsets(axes):
    found = [{}]
    for axis in axes:
        found = [dict(o, **{axis: i}) for o in found for i in range(PARTS[axis])]
    found = [o for o in found if any(o.values())]

    def distance(o):
        total = 0
        for axis, i in o.items():
            if axis in ("x", "y"):
                total += min(i, 4 - i)
            elif axis == "zh":
                total += 2 * i
            else:
                total += i
        return total

    return sorted(found, key=lambda o: -distance(o))


GROUP_A = offsets(("zl", "zh", "c"))
GROUP_B = offsets(("x", "y"))
EVERYONE = offsets(("x", "y", "zh", "zl", "c"))


def kernel(cot, speed, coeff, dirs, out, cfield, cf, vel, y4, w4, g4, qr4, y3, w3, g3, qr3, y2, w2, t1, t2, b1,
           signs, sums, load_sem, send, recv, ar_send, ar_recv, in_sem, out_sem):
    gx, gy = lax.axis_index("gx"), lax.axis_index("gy")
    place = {"zl": gx // 4, "y": gx % 4, "x": gy // 4, "zh": (gy // 2) % 2, "c": gy % 2}

    def device(offset):
        at = {k: (place[k] + offset[k]) % PARTS[k] if offset.get(k, 0) else place[k] for k in place}
        return {"gx": at["zl"] * 4 + at["y"], "gy": at["x"] * 4 + at["zh"] * 2 + at["c"]}

    def neighbour(sx, sy):
        return {"gx": (gx + sx + 8) % 8, "gy": (gy + sy + 16) % 16}

    lane = lax.broadcasted_iota(jnp.int32, (8, BZ), 1)

    def zero_rim(ref, *lead):
        for x in (0, 1, EX - 2, EX - 1):
            ref[(*lead, x)] = jnp.zeros((EY, BZ), F32)

        def body(x, _):
            ref[(*lead, x, pl.ds(TOP - 8, 8))] = jnp.zeros((8, BZ), F32)
            ref[(*lead, x, pl.ds(BOT, 8))] = jnp.zeros((8, BZ), F32)
            return 0

        lax.fori_loop(OX, OX + BX, body, 0, unroll=8)

    inner = (pl.ds(OX, BX), pl.ds(OY, BY))
    loads = [pltpu.make_async_copy(cot, cfield.at[inner], load_sem.at[0])]
    for d in range(3):
        loads.append(pltpu.make_async_copy(speed.at[d], vel.at[(d, *inner)], load_sem.at[1 + d]))
    for d in range(3):
        loads.append(pltpu.make_async_copy(coeff.at[d], cf.at[(d, *inner)], load_sem.at[4 + d]))
    for load in loads:
        load.start()

    zero_rim(cfield)
    for d in range(3):
        zero_rim(cf, d)
    zero_rim(vel, 0)
    zero_rim(vel, 1)
    zero_rim(y4)

    barrier = pltpu.get_barrier_semaphore()
    friends = [neighbour(sx, sy) for sx in (-1, 0, 1) for sy in (-1, 0, 1) if sx or sy]
    friends += [device(o) for o in GROUP_A] + [device(o) for o in GROUP_B]
    for friend in friends:
        pl.semaphore_signal(barrier, inc=1, device_id=friend, device_id_type=MESH)

    for k in range(2):
        zero_rim(qr4, k)
    for k in range(3):
        zero_rim(qr3, k)

    signs[...] = jnp.zeros((128, 128), F32)
    for d in range(3):
        signs[pl.ds(32 * d, 32), pl.ds(0, 64)] = (1 - 2 * dirs[d]).astype(F32)
    signs[...] = signs[...].T
    for load in loads[1:4]:
        load.wait()
    columns = signs[pl.ds(0, 64), :]
    for d in range(3):
        for x in range(BX):
            k = 32 * d + x
            rows = pl.ds(OY, BY)
            vel[d, OX + x, rows] = vel[d, OX + x, rows] * columns[:, k:k + 1]
    loads[0].wait()
    for load in loads[4:]:
        load.wait()

    count = [0]
    edges = {-1: (gx > 0, gy > 0), 1: (gx < 7, gy < 15)}

    def transfer(ref, lead, source, target, sx, sy):
        k = count[0]
        count[0] += 1
        copy = pltpu.make_async_remote_copy(
            src_ref=ref.at[(*lead, *source)], dst_ref=ref.at[(*lead, *target)],
            send_sem=send.at[k], recv_sem=recv.at[k], device_id=neighbour(sx, sy), device_id_type=MESH)
        sends, receives = None, None
        if sx:
            sends, receives = edges[sx][0], edges[-sx][0]
        if sy:
            ys, yr = edges[sy][1], edges[-sy][1]
            sends = ys if sends is None else jnp.logical_and(sends, ys)
            receives = yr if receives is None else jnp.logical_and(receives, yr)
        pl.when(sends)(copy.start)
        return copy, sends, receives

    def finish(copies):
        for copy, sends, receives in copies:
            pl.when(receives)(copy.wait_recv)
            pl.when(sends)(copy.wait_send)

    XS, YS = pl.ds(OX, BX), pl.ds(OY, BY)

    def to_above(ref, lead, axis, width):
        if axis == 0:
            return transfer(ref, lead, (pl.ds(OX + BX - width, width), YS), (pl.ds(OX - width, width), YS), 1, 0)
        return transfer(ref, lead, (XS, pl.ds(BOT - width, width)), (XS, pl.ds(TOP - width, width)), 0, 1)

    def to_below(ref, lead, axis, width):
        if axis == 0:
            return transfer(ref, lead, (pl.ds(OX, width), YS), (pl.ds(OX + BX, width), YS), -1, 0)
        return transfer(ref, lead, (XS, pl.ds(TOP, width)), (XS, pl.ds(BOT, width)), 0, -1)

    def corner(ref, lead, sx, sy):
        xs, xt = (OX + BX - 1, OX - 1) if sx > 0 else (OX, OX + BX)
        ys, yt = (BOT - 1, TOP - 1) if sy > 0 else (TOP, BOT)
        return transfer(ref, lead, (pl.ds(xs, 1), pl.ds(ys, 1)), (pl.ds(xt, 1), pl.ds(yt, 1)), sx, sy)

    def swap(ref, lead):
        return [to_above(ref, lead, 0, 2), to_below(ref, lead, 0, 2), to_above(ref, lead, 1, 2),
                to_below(ref, lead, 1, 2)] + [corner(ref, lead, sx, sy) for sx in (1, -1) for sy in (1, -1)]

    def ahead_z(v):
        rows = v.shape[0]
        at = lax.broadcasted_iota(jnp.int32, (rows, BZ), 1)
        return jnp.where(at == BZ - 1, 0.0, pltpu.roll(v, BZ - 1, 1))

    def behind_z(v):
        rows = v.shape[0]
        at = lax.broadcasted_iota(jnp.int32, (rows, BZ), 1)
        return jnp.where(at == 0, 0.0, pltpu.roll(v, 1, 1))

    def stencil(src, x0, n, segments, emit, advect=True, diffuse=True, unroll=1):
        def start(r, size):
            rows = pl.ds(r, size)
            v = src[x0, rows]
            dx = v - src[x0 - 1, rows]
            parts = [v]
            if diffuse:
                parts.append(cf[0, x0 - 1, rows] * dx)
            if advect:
                parts.append(jnp.minimum(vel[0, x0 - 1, rows], 0.0) * dx)
            return tuple(parts)

        def plane(x, carry):
            done = []
            for (r, size), held in zip(segments, carry):
                rows, up, down = pl.ds(r, size), pl.ds(r + 1, size), pl.ds(r - 1, size)
                v = held[0]
                ahead = src[x + 1, rows]
                dx = ahead - v
                dyu = src[x, up] - v
                dyd = v - src[x, down]
                dz = ahead_z(v) - v
                parts = [ahead]
                dv = fv = None
                if diffuse:
                    fx = cf[0, x, rows] * dx
                    fz = cf[2, x, rows] * dz
                    dv = (fx - held[1]) + (cf[1, x, rows] * dyu - cf[1, x, down] * dyd) + (fz - behind_z(fz))
                    parts.append(fx)
                if advect:
                    u0, u1, u2 = vel[0, x, rows], vel[1, x, rows], vel[2, x, rows]
                    fv = (jnp.maximum(u0, 0.0) * dx + held[-1])
                    fv = fv + (jnp.maximum(u1, 0.0) * dyu + jnp.minimum(vel[1, x, down], 0.0) * dyd)
                    fv = fv + (jnp.maximum(u2, 0.0) * dz + behind_z(jnp.minimum(u2, 0.0) * dz))
                    parts.append(jnp.minimum(u0, 0.0) * dx)
                emit(x, rows, v, fv, dv)
                done.append(tuple(parts))
            return tuple(done)

        carry = tuple(start(r, size) for r, size in segments)
        if unroll >= n:
            for i in range(n):
                carry = plane(x0 + i, carry)
        else:
            lax.fori_loop(x0, x0 + n, plane, carry, unroll=unroll)

    WHOLE = ((OY, BY),)
    INNER = ((OY + 8, BY - 16),)
    STRIPS = ((OY, 8), (BOT - 8, 8))

    def rim_then_inner(run, width):
        run(OX, width, WHOLE, width)
        run(OX + BX - width, width, WHOLE, width)
        run(OX + width, BX - 2 * width, STRIPS, BX)

    def inner_part(run, width):
        n = BX - 2 * width
        run(OX + width, n, INNER, n // 4 if n % 4 == 0 else n // 5)

    def emit_y4(x, rows, v, fv, dv):
        y4[x, rows] = 0.25 * (fv + dv)

    def run_y4(x0, n, segments, unroll):
        stencil(cfield, x0, n, segments, emit_y4, unroll=unroll)

    pl.semaphore_wait(barrier, len(friends))
    first = [to_above(cfield, (), 0, 1), to_below(cfield, (), 0, 1), to_above(cfield, (), 1, 1),
             to_below(cfield, (), 1, 1), to_above(cf, (0,), 0, 2), to_above(cf, (1,), 1, 2),
             to_above(vel, (0,), 0, 1), to_above(vel, (1,), 1, 1)]
    later = [to_above(cf, (pl.ds(1, 2),), 0, 1), to_below(cf, (pl.ds(0, 3),), 0, 1),
             to_above(cf, (0,), 1, 1), to_above(cf, (2,), 1, 1), to_below(cf, (pl.ds(0, 3),), 1, 1),
             corner(cf, (pl.ds(0, 2),), 1, 1), corner(cf, (1,), -1, 1), corner(cf, (0,), 1, -1)]
    for o in GROUP_B:
        pl.semaphore_signal(in_sem, inc=1, device_id=device(o), device_id_type=MESH)
    inner_part(run_y4, 1)
    finish(first)
    rim_then_inner(run_y4, 1)
    moved = swap(y4, ())

    def laplacian(src, dst, x0, n, segments, unroll):
        def emit(x, rows, v, fv, dv):
            dst[x, rows] = -dv

        stencil(src, x0, n, segments, emit, advect=False, unroll=unroll)

    WIDE = ((OY - 8, BY + 16),)

    def clear_outside(ref):
        @pl.when(gx == 0)
        def _():
            ref[OX - 1] = jnp.zeros((EY, BZ), F32)

        @pl.when(gx == 7)
        def _():
            ref[OX + BX] = jnp.zeros((EY, BZ), F32)

        def rows_at(r):
            def body(x, _):
                ref[x, pl.ds(r, 8)] = jnp.zeros((8, BZ), F32)
                return 0
            lax.fori_loop(OX, OX + BX, body, 0, unroll=8)

        pl.when(gy == 0)(lambda: rows_at(TOP - 8))
        pl.when(gy == 15)(lambda: rows_at(BOT))

    def fold(values):
        return jnp.sum(values.reshape(values.shape[0] // 8, 8, BZ), axis=0)

    def moments(y, w):
        def plane(x, carry):
            a0, a1, a2, a3, here = carry
            rows = pl.ds(OY, BY)
            v = y[x, rows]
            ahead = w[x + 1, rows]
            dx = ahead - here
            dy = w[x, pl.ds(OY + 1, BY)] - here
            dz = ahead_z(here) - here
            energy = (cf[0, x, rows] * dx) * dx + (cf[1, x, rows] * dy) * dy + (cf[2, x, rows] * dz) * dz
            return (a0 + fold(v * v), a1 + fold(v * here), a2 + fold(here * here), a3 + fold(energy), ahead)

        zero = jnp.zeros((8, BZ), F32)
        got = lax.fori_loop(OX, OX + BX, plane, (zero, zero, zero, zero, w[OX, pl.ds(OY, BY)]), unroll=4)
        return got[:4]

    def send_sums(r, parts):
        row = jnp.zeros((1, BZ), F32)
        for k, part in enumerate(parts):
            total = jnp.sum(jnp.sum(part, axis=0, keepdims=True), axis=1, keepdims=True)
            row = jnp.where(lane[0:1] == k, total, row)
        sums[r, pl.ds(127, 1)] = row
        for k, o in enumerate(EVERYONE):
            pltpu.make_async_remote_copy(
                src_ref=sums.at[r, pl.ds(127, 1)], dst_ref=sums.at[r, pl.ds(k, 1)],
                send_sem=ar_send.at[r], recv_sem=ar_recv.at[r], device_id=device(o), device_id_type=MESH).start()

    def solve(r):
        pltpu.make_async_remote_copy(
            src_ref=sums.at[r, pl.ds(0, 127)], dst_ref=sums.at[r, pl.ds(0, 127)],
            send_sem=ar_send.at[r], recv_sem=ar_recv.at[r], device_id=device(EVERYONE[0]), device_id_type=MESH).wait()
        row = jnp.sum(sums[r], axis=0, keepdims=True)
        m0, k1, k2, k3 = (
            jnp.broadcast_to(jnp.sum(jnp.where(lane[0:1] == k, row, 0.0), axis=1, keepdims=True), (8, BZ))
            for k in range(4))
        h = 0.25
        alpha = m0 / (m0 + h * k1)
        rho = k1 / m0
        ss = k2 - rho * k1
        sls = k3 - 2.0 * rho * k2 + rho * (rho * k1)
        beta = (alpha * h) * (alpha * h) * (ss / m0)
        under = ss * (1.0 - beta / alpha) + h * sls
        second = jnp.where(under > 0.0, jnp.clip(ss / under, 0.0, 1.0), 0.0)
        return alpha + second * (alpha * h * rho + beta), -second * alpha * h

    def full(scalar, size):
        return jnp.concatenate([scalar] * (size // 8), axis=0)

    def advance(y, w, qr, g, r):
        def emit_q(x, rows, v, fv, dv):
            qr[0, x, rows] = 0.5 * fv - 0.25 * w[x, rows]

        def emit_r(x, rows, v, fv, dv):
            qr[1, x, rows] = 0.5 * fv + 0.25 * dv
            g[x, rows] = dv

        def run_q(x0, n, segments, unroll):
            stencil(y, x0, n, segments, emit_q, diffuse=False, unroll=unroll)

        def run_r(x0, n, segments, unroll):
            stencil(w, x0, n, segments, emit_r, unroll=unroll)

        rim_then_inner(run_q, 2)
        rim_then_inner(run_r, 2)
        copies = swap(qr, (pl.ds(0, 2),))
        inner_part(run_q, 2)
        inner_part(run_r, 2)
        return copies

    def everywhere(fn):
        def body(x, _):
            fn(x, pl.ds(OY - 8, BY + 16))
            return 0
        lax.fori_loop(0, EX, body, 0, unroll=4)

    def block(fn, unroll=4):
        def body(x, _):
            fn(x, pl.ds(OY, BY))
            return 0
        lax.fori_loop(OX, OX + BX, body, 0, unroll=unroll)

    inner_part(functools.partial(laplacian, y4, w4), 1)
    finish(moved)
    finish(later)
    laplacian(y4, w4, OX - 1, 2, WIDE, 2)
    laplacian(y4, w4, OX + BX - 1, 2, WIDE, 2)
    laplacian(y4, w4, OX + 1, BX - 2, ((OY - 8, 16), (BOT - 8, 16)), BX)
    clear_outside(w4)
    parts = moments(y4, w4)
    pl.semaphore_wait(in_sem, len(GROUP_B))
    send_sums(0, parts)
    moved = advance(y4, w4, qr4, g4, 0)
    finish(moved)
    a4, c4 = solve(0)

    def base2(x, rows):
        size = rows.size
        a, c = full(a4, size), full(c4, size)
        qr3[2, x, rows] = (1.4 * y4[x, rows] + a * (0.6 * qr4[0, x, rows] - 0.2 * w4[x, rows])
                           + c * (0.6 * qr4[1, x, rows] + 0.2 * g4[x, rows]))

    block(base2)
    moved2 = swap(qr3, (2,))

    def make_y3(x, rows):
        a, c = full(a4, rows.size), full(c4, rows.size)
        y3[x, rows] = y4[x, rows] + a * qr4[0, x, rows] + c * qr4[1, x, rows]

    everywhere(make_y3)
    laplacian(y3, w3, OX - 1, BX + 2, WIDE, 4)
    clear_outside(w3)
    send_sums(1, moments(y3, w3))
    moved = advance(y3, w3, qr3, g3, 1)
    finish(moved2)
    finish(moved)
    a3, c3 = solve(1)

    def make_y2(x, rows):
        a, c = full(a3, rows.size), full(c3, rows.size)
        y2[x, rows] = qr3[2, x, rows] + a * qr3[0, x, rows] + c * qr3[1, x, rows]

    everywhere(make_y2)
    laplacian(y2, w2, OX - 1, BX + 2, WIDE, 4)
    clear_outside(w2)
    send_sums(2, moments(y2, w2))

    def emit_t1(x, rows, v, fv, dv):
        t1[x - OX, pl.ds(rows.start - OY, rows.size)] = v + 0.5 * fv - 0.25 * w2[x, rows]

    def emit_t2(x, rows, v, fv, dv):
        t2[x - OX, pl.ds(rows.start - OY, rows.size)] = v + 0.5 * fv + 0.25 * dv

    stencil(y2, OX, BX, WHOLE, emit_t1, diffuse=False, unroll=4)
    stencil(w2, OX, BX, WHOLE, emit_t2, unroll=4)

    def base1(x, rows):
        size = rows.size
        a, c, a_, c_ = full(a4, size), full(c4, size), full(a3, size), full(c3, size)
        total = cfield[x, rows] + 0.6 * y4[x, rows]
        total = total + a * (y4[x, rows] + 0.4 * qr4[0, x, rows] - 0.05 * w4[x, rows])
        total = total + c * (w4[x, rows] + 0.4 * qr4[1, x, rows] + 0.05 * g4[x, rows])
        total = total + a_ * (y3[x, rows] + 0.5 * qr3[0, x, rows] - 0.125 * w3[x, rows])
        total = total + c_ * (w3[x, rows] + 0.5 * qr3[1, x, rows] + 0.125 * g3[x, rows])
        b1[x - OX] = total

    block(base1)
    a2, c2 = solve(2)
    stores = []
    for k in range(4):
        planes = pl.ds(8 * k, 8)

        def body(x, _):
            b1[x] = b1[x] + full(a2, BY) * t1[x] + full(c2, BY) * t2[x]
            return 0

        lax.fori_loop(8 * k, 8 * k + 8, body, 0, unroll=4)
        store = pltpu.make_async_copy(b1.at[planes], out.at[planes], out_sem.at[k])
        store.start()
        stores.append(store)
    for store in stores:
        store.wait()


COPIES = 80


def local(cotangent, speed, coeff, dirs):
    ext = pltpu.VMEM(EXT, F32)
    plain = pltpu.VMEM((BX, BY, BZ), F32)

    def stack(n):
        return pltpu.VMEM((n, *EXT), F32)

    anywhere = pl.BlockSpec(memory_space=pl.ANY)
    return pl.pallas_call(
        kernel,
        name="adjoint_step",
        out_shape=jax.ShapeDtypeStruct((BX, BY, BZ), F32),
        in_specs=[anywhere, anywhere, anywhere, pl.BlockSpec(memory_space=pltpu.VMEM)],
        out_specs=anywhere,
        scratch_shapes=[
            ext, stack(3), stack(3), ext, ext, ext, stack(2), ext, ext, ext, stack(3), ext, ext,
            plain, plain, plain, pltpu.VMEM((128, 128), F32), pltpu.VMEM((3, 128, BZ), F32),
            pltpu.SemaphoreType.DMA((7,)), pltpu.SemaphoreType.DMA((COPIES,)), pltpu.SemaphoreType.DMA((COPIES,)),
            pltpu.SemaphoreType.DMA((3,)), pltpu.SemaphoreType.DMA((3,)), pltpu.SemaphoreType.REGULAR,
            pltpu.SemaphoreType.DMA((4,)),
        ],
        compiler_params=pltpu.CompilerParams(
            collective_id=0, has_side_effects=True, vmem_limit_bytes=60 * 1024 * 1024),
    )(cotangent, speed, coeff, dirs)


def solution(mesh):
    placed = (P("gx", "gy", None), P(None, "gx", "gy", None), P(None, "gx", "gy", None), P(None, "gx", "gy"))
    return jax.shard_map(local, mesh=mesh, in_specs=placed, out_specs=P("gx", "gy", None), check_vma=False)
```

time: 493 us -> 61.3 us (0.12); the launches traced: 487 us -> 61.1 us
  blocking collectives: 243 us -> 0 us
  starting transfers between devices: 117 us -> 0 us
  other arithmetic: 80.7 us -> 0 us
  Pallas kernels: 0 us -> 58.8 us
  waiting for transfers between devices: 24.1 us -> 0 us
  between operations: 18.6 us -> 0.01 us
    psum x30 -> x0, blocking collectives: 243 us -> none  [by_axis(): array = lax.psum(array, axis)]
    ppermute x42 -> x0, starting transfers between devices: 117 us -> none  [the longest x20 73.2 us: padded(): lax.ppermute(last, axis, up)]
    pallas_call x0 -> x1, Pallas kernels: none -> 58.8 us  [local(): pl.pallas_call(kernel, name='adjoint_step', out_shape=jax.ShapeDtypeStruc...]
    reduce_sum x9 -> x0, other arithmetic: 27.6 us -> none  [the longest x6 19.8 us: paired_products(): jnp.sum(residual * image)]
    ppermute x42 -> x0, waiting for transfers between devices: 24.1 us -> none  [the longest x20 22.2 us: padded(): lax.ppermute(leading, axis, [(b, a) for a, b in up])]
    add x4 -> x0, other arithmetic: 21.5 us -> none  [the longest x3 14.6 us: apply_halo(): total = total + jnp.where(velocity_low[dimension] > 0, 0.0, moved_low)]
    another operation x17 -> x0, other arithmetic: 21.1 us -> none  [the longest x15 21.1 us: local(): source = operate(jnp.stack([advected, diffused]))]
    concatenate x4 -> x0, other arithmetic: 7.94 us -> none  [padded(): jnp.concatenate([jnp.pad(low, around), array, jnp.pad(high, around)], axi...]
  transfers between devices with their start and end apart: 42 -> 0, of which waited for: 10 -> 0; matrix products, arithmetic and copies ran while one was open for 3% -> 0% of each run, Pallas kernels for 0% -> 0%
where the time goes in v1:
time: 61.3 us; the launch traced here: 61.1 us
  Pallas kernels  58.8 us (96%)
  local copies, waits for them, and re-layouts  2.31 us (4%)
    pallas_call x1, Pallas kernels, local(): pl.pallas_call(kernel, name='adjoint_step', out_shape=jax.ShapeDtypeStruc...  58.8 us
    unnamed x1, local copies, waits for them, and re-layouts  2.31 us

profile of v1, /device:TPU:1, one launch (start us, length us, event | category | flops | bytes accessed | tf_op | source)
XLA Modules:
  0.0 61.1 jit_solution(7748839595284807519)
XLA Ops:
  0.0 58.8 %adjoint_step.1 = f32[32,64,128]{2,1,0:T(8,128)} custom-call(f32[32,64,128]{2,1,0:T(8,128)} %cot.1, f32[3,32,64,128]{3,2,1,0:T(8,128)} %speed.1, f32[3,32,64,128]{3,2,1,0:T(8,128)} %coeff.1, s32[3,32,64]{2,1,0:T(8,128)} %dirs.1), custom_call_target="tpu_custom_call" | custom-call | tf_op jit(solution)/shard_map/adjoint_step/pallas_call | solution.py:451
  58.8 2.3 %copy.6 = f32[32,64,128]{2,1,0:T(8,128)} copy(f32[32,64,128]{2,1,0:T(8,128)} %adjoint_step.1) | data formatting | bytes 2097152

commit v2 on v1

--- a/solution.py
+++ b/solution.py
@@ -9,10 +9,12 @@
 
 MESH = pl.DeviceIdType.MESH
 F32 = jnp.float32
+UNROLL = (28, 34, 16)
+UI, UL, UT = (6, 7), 4, 4
 
 BX, BY, BZ = 32, 64, 128
 OX, OY = 2, 16
-EX, EY = BX + 2 * OX, BY + 2 * OY
+NX, EX, EY = BX + 2 * OX, BX + 2 * OX, BY + 2 * OY
 TOP, BOT = OY, OY + BY
 EXT = (EX, EY, BZ)
 PARTS = {"zl": 2, "y": 4, "x": 4, "zh": 2, "c": 2}
@@ -43,8 +45,8 @@
 EVERYONE = offsets(("x", "y", "zh", "zl", "c"))
 
 
-def kernel(cot, speed, coeff, dirs, out, cfield, cf, vel, y4, w4, g4, qr4, y3, w3, g3, qr3, y2, w2, t1, t2, b1,
-           signs, sums, load_sem, send, recv, ar_send, ar_recv, in_sem, out_sem):
+def kernel(cot, speed, coeff, dirs, out, cfield, cf, vel, y4, w4, g4, qr4, y3, w3, g3, qr3, y2, w2, t1, t2, b1, sc, up_z, down_z, centre,
+           signs, sums, load_sem, send, recv, ar_send, ar_recv, in_sem):
     gx, gy = lax.axis_index("gx"), lax.axis_index("gy")
     place = {"zl": gx // 4, "y": gx % 4, "x": gy // 4, "zh": (gy // 2) % 2, "c": gy % 2}
 
@@ -58,7 +60,7 @@
     lane = lax.broadcasted_iota(jnp.int32, (8, BZ), 1)
 
     def zero_rim(ref, *lead):
-        for x in (0, 1, EX - 2, EX - 1):
+        for x in (0, 1, NX - 2, NX - 1):
             ref[(*lead, x)] = jnp.zeros((EY, BZ), F32)
 
         def body(x, _):
@@ -212,24 +214,63 @@
         else:
             lax.fori_loop(x0, x0 + n, plane, carry, unroll=unroll)
 
+    def blocks(src, x0, n, px, segments, emit, advect=True, diffuse=True):
+        def at(ref, lead, x, count, r, size):
+            return ref[(*lead, pl.ds(x, count), pl.ds(r, size))].reshape(count * size, BZ)
+
+        def one(x):
+            for r, size in segments:
+                wide = at(src, (), x - 1, px + 2, r, size)
+                v = wide[size:-size]
+                dx = wide[size:] - wide[:-size]
+                dyu = at(src, (), x, px, r + 1, size) - v
+                dyd = v - at(src, (), x, px, r - 1, size)
+                dz = ahead_z(v) - v
+                dv = fv = None
+                if diffuse:
+                    fx = at(cf, (0,), x - 1, px + 1, r, size) * dx
+                    fz = at(cf, (2,), x, px, r, size) * dz
+                    fy = at(cf, (1,), x, px, r, size) * dyu - at(cf, (1,), x, px, r - 1, size) * dyd
+                    dv = (fx[size:] - fx[:-size]) + fy + (fz - behind_z(fz))
+                if advect:
+                    u0 = at(vel, (0,), x - 1, px + 1, r, size)
+                    u1, u2 = at(vel, (1,), x, px, r, size), at(vel, (2,), x, px, r, size)
+                    u1d = at(vel, (1,), x, px, r - 1, size)
+                    fv = jnp.maximum(u0[size:], 0.0) * dx[size:] + jnp.minimum(u0[:-size], 0.0) * dx[:-size]
+                    fv = fv + (jnp.maximum(u1, 0.0) * dyu + jnp.minimum(u1d, 0.0) * dyd)
+                    fv = fv + (jnp.maximum(u2, 0.0) * dz + behind_z(jnp.minimum(u2, 0.0) * dz))
+                emit(pl.ds(x, px), pl.ds(r, size), v, fv, dv)
+
+        if n == px:
+            one(x0)
+        else:
+            lax.fori_loop(0, n // px, lambda i, _: (one(x0 + i * px), 0)[1], 0)
+
+    def shaped(x, rows, value):
+        return value.reshape(x.size, rows.size, BZ) if isinstance(x, pl.Slice) else value
+
+    def flat(value):
+        return value.reshape(-1, BZ)
+
     WHOLE = ((OY, BY),)
     INNER = ((OY + 8, BY - 16),)
     STRIPS = ((OY, 8), (BOT - 8, 8))
-
-    def rim_then_inner(run, width):
-        run(OX, width, WHOLE, width)
-        run(OX + BX - width, width, WHOLE, width)
-        run(OX + width, BX - 2 * width, STRIPS, BX)
-
-    def inner_part(run, width):
+    CORE = tuple((OY + 8 + 24 * i, 24) for i in range(2))
+    WIDE7 = tuple((OY - 8 + 40 * i, 40) for i in range(2))
+    HALVES = ((OY, BY // 2), (OY + BY // 2, BY // 2))
+
+    def rim(src, emit, width, **kinds):
+        ends = HALVES if width == 2 else WHOLE
+        blocks(src, OX, width, width, ends, emit, **kinds)
+        blocks(src, OX + BX - width, width, width, ends, emit, **kinds)
+        blocks(src, OX + width, BX - 2 * width, 10 if width == 1 else 7, STRIPS, emit, **kinds)
+
+    def inner_part(src, emit, width, **kinds):
         n = BX - 2 * width
-        run(OX + width, n, INNER, n // 4 if n % 4 == 0 else n // 5)
+        stencil(src, OX + width, n, INNER, emit, unroll=UI[width - 1], **kinds)
 
     def emit_y4(x, rows, v, fv, dv):
-        y4[x, rows] = 0.25 * (fv + dv)
-
-    def run_y4(x0, n, segments, unroll):
-        stencil(cfield, x0, n, segments, emit_y4, unroll=unroll)
+        y4[x, rows] = shaped(x, rows, 0.25 * (fv + dv))
 
     pl.semaphore_wait(barrier, len(friends))
     first = [to_above(cfield, (), 0, 1), to_below(cfield, (), 0, 1), to_above(cfield, (), 1, 1),
@@ -240,16 +281,15 @@
              corner(cf, (pl.ds(0, 2),), 1, 1), corner(cf, (1,), -1, 1), corner(cf, (0,), 1, -1)]
     for o in GROUP_B:
         pl.semaphore_signal(in_sem, inc=1, device_id=device(o), device_id_type=MESH)
-    inner_part(run_y4, 1)
+    inner_part(cfield, emit_y4, 1)
     finish(first)
-    rim_then_inner(run_y4, 1)
+    rim(cfield, emit_y4, 1)
     moved = swap(y4, ())
 
-    def laplacian(src, dst, x0, n, segments, unroll):
+    def to_w(dst):
         def emit(x, rows, v, fv, dv):
-            dst[x, rows] = -dv
-
-        stencil(src, x0, n, segments, emit, advect=False, unroll=unroll)
+            dst[x, rows] = shaped(x, rows, -dv)
+        return emit
 
     WIDE = ((OY - 8, BY + 16),)
 
@@ -275,19 +315,21 @@
         return jnp.sum(values.reshape(values.shape[0] // 8, 8, BZ), axis=0)
 
     def moments(y, w):
-        def plane(x, carry):
-            a0, a1, a2, a3, here = carry
-            rows = pl.ds(OY, BY)
-            v = y[x, rows]
-            ahead = w[x + 1, rows]
-            dx = ahead - here
-            dy = w[x, pl.ds(OY + 1, BY)] - here
-            dz = ahead_z(here) - here
-            energy = (cf[0, x, rows] * dx) * dx + (cf[1, x, rows] * dy) * dy + (cf[2, x, rows] * dz) * dz
-            return (a0 + fold(v * v), a1 + fold(v * here), a2 + fold(here * here), a3 + fold(energy), ahead)
-
         zero = jnp.zeros((8, BZ), F32)
-        got = lax.fori_loop(OX, OX + BX, plane, (zero, zero, zero, zero, w[OX, pl.ds(OY, BY)]), unroll=4)
+        got = (zero,) * 4
+        for r, size in HALVES:
+            def plane(x, carry, r=r, size=size):
+                a0, a1, a2, a3, here = carry
+                rows = pl.ds(r, size)
+                v = y[x, rows]
+                ahead = w[x + 1, rows]
+                dx = ahead - here
+                dy = w[x, pl.ds(r + 1, size)] - here
+                dz = ahead_z(here) - here
+                energy = (cf[0, x, rows] * dx) * dx + (cf[1, x, rows] * dy) * dy + (cf[2, x, rows] * dz) * dz
+                return (a0 + fold(v * v), a1 + fold(v * here), a2 + fold(here * here), a3 + fold(energy), ahead)
+
+            got = lax.fori_loop(OX, OX + BX, plane, (*got[:4], w[OX, pl.ds(r, size)]), unroll=16)
         return got[:4]
 
     def send_sums(r, parts):
@@ -322,32 +364,113 @@
     def full(scalar, size):
         return jnp.concatenate([scalar] * (size // 8), axis=0)
 
-    def advance(y, w, qr, g, r):
-        def emit_q(x, rows, v, fv, dv):
-            qr[0, x, rows] = 0.5 * fv - 0.25 * w[x, rows]
-
-        def emit_r(x, rows, v, fv, dv):
-            qr[1, x, rows] = 0.5 * fv + 0.25 * dv
-            g[x, rows] = dv
-
-        def run_q(x0, n, segments, unroll):
-            stencil(y, x0, n, segments, emit_q, diffuse=False, unroll=unroll)
-
-        def run_r(x0, n, segments, unroll):
-            stencil(w, x0, n, segments, emit_r, unroll=unroll)
-
-        rim_then_inner(run_q, 2)
-        rim_then_inner(run_r, 2)
+    def held(ref, x, px, r, size, dx=0, dr=0):
+        return ref[pl.ds(x + dx, px), pl.ds(r + dr, size)].reshape(px * size, BZ)
+
+    def d_weights(x, px, r, size):
+        return (held(cf.at[0], x, px, r, size), held(cf.at[0], x, px, r, size, -1),
+                held(cf.at[1], x, px, r, size), held(cf.at[1], x, px, r, size, 0, -1),
+                held(up_z, x, px, r, size), held(down_z, x, px, r, size), held(centre, x, px, r, size))
+
+    def s_weights(x, px, r, size):
+        return tuple(held(sc.at[k], x, px, r, size, -OX, -OY) for k in range(7))
+
+    def seven(src, weights, emit, x, px, r, size, before, here, after):
+        north, south = held(src, x, px, r, size, 0, 1), held(src, x, px, r, size, 0, -1)
+        up, down = pltpu.roll(here, BZ - 1, 1), pltpu.roll(here, 1, 1)
+        results = []
+        for weight in weights:
+            e, w, n, s, u, d, c = weight(x, px, r, size)
+            results.append((e * after + w * before) + (n * north + s * south) + (u * up + d * down) - c * here)
+        emit(x, px, r, size, here, *results)
+
+    def sweep7(src, x0, n, segments, weights, emit, unroll):
+        for r, size in segments:
+            def plane(x, carry, r=r, size=size):
+                before, here = carry
+                after = held(src, x, 1, r, size, 1)
+                seven(src, weights, emit, x, 1, r, size, before, here, after)
+                return here, after
+
+            lax.fori_loop(x0, x0 + n, plane, (held(src, x0, 1, r, size, -1), held(src, x0, 1, r, size)), unroll=unroll)
+
+    def blocks7(src, x0, n, px, segments, weights, emit):
+        def one(x):
+            for r, size in segments:
+                wide = held(src, x - 1, px + 2, r, size)
+                seven(src, weights, emit, x, px, r, size, wide[:-2 * size], wide[size:-size], wide[2 * size:])
+
+        if n == px:
+            one(x0)
+        else:
+            lax.fori_loop(0, n // px, lambda i, _: (one(x0 + i * px), 0)[1], 0)
+
+    def put(ref, x, px, r, size, value, dx=0, dr=0):
+        ref[pl.ds(x + dx, px), pl.ds(r + dr, size)] = value.reshape(px, size, BZ)
+
+    def advance(y, w, qr, g):
+        def emit_q(x, px, r, size, v, sv):
+            put(qr.at[0], x, px, r, size, sv)
+
+        def emit_r(x, px, r, size, v, sv, dv):
+            put(qr.at[1], x, px, r, size, sv)
+            put(g, x, px, r, size, dv)
+
+        def rim7(src, weights, emit):
+            blocks7(src, OX, 2, 2, HALVES, weights, emit)
+            blocks7(src, OX + BX - 2, 2, 2, HALVES, weights, emit)
+            blocks7(src, OX + 2, BX - 4, 7, STRIPS, weights, emit)
+
+        both = (s_weights, d_weights)
+        rim7(y, (s_weights,), emit_q)
+        rim7(w, both, emit_r)
         copies = swap(qr, (pl.ds(0, 2),))
-        inner_part(run_q, 2)
-        inner_part(run_r, 2)
+        sweep7(y, OX + 2, BX - 4, CORE, (s_weights,), emit_q, UNROLL[0])
+        sweep7(w, OX + 2, BX - 4, CORE, both, emit_r, UNROLL[0])
         return copies
+
+    def laplacian7(src, dst):
+        def emit(x, px, r, size, v, dv):
+            put(dst, x, px, r, size, -dv)
+
+        sweep7(src, OX - 1, BX + 2, WIDE7, (d_weights,), emit, UNROLL[1])
+
+    def prepare_s():
+        def body(x, _):
+            for r, size in HALVES:
+                a = [vel[d, x, pl.ds(r, size)] for d in range(3)]
+                k = [0.25 * cf[d, x, pl.ds(r, size)] for d in range(3)]
+                e, n, u = (0.5 * jnp.maximum(a[d], 0.0) + k[d] for d in range(3))
+                w = 0.25 * cf[0, x - 1, pl.ds(r, size)] - 0.5 * jnp.minimum(vel[0, x - 1, pl.ds(r, size)], 0.0)
+                s = 0.25 * cf[1, x, pl.ds(r - 1, size)] - 0.5 * jnp.minimum(vel[1, x, pl.ds(r - 1, size)], 0.0)
+                d = behind_z(k[2] - 0.5 * jnp.minimum(a[2], 0.0))
+                at = lax.broadcasted_iota(jnp.int32, (size, BZ), 1)
+                values = (e, w, n, s, jnp.where(at == BZ - 1, 0.0, u), d, (e + w) + (n + s) + (u + d))
+                for i, value in enumerate(values):
+                    sc[i, x - OX, pl.ds(r - OY, size)] = value
+            return 0
+
+        lax.fori_loop(OX, OX + BX, body, 0, unroll=2)
+
+    def prepare_d(x0, n, r, size):
+        def body(x, _):
+            rows = pl.ds(r, size)
+            k = cf[2, x, rows]
+            d = behind_z(k)
+            at = lax.broadcasted_iota(jnp.int32, (size, BZ), 1)
+            up_z[x, rows] = jnp.where(at == BZ - 1, 0.0, k)
+            down_z[x, rows] = d
+            centre[x, rows] = ((cf[0, x, rows] + cf[0, x - 1, rows]) + (cf[1, x, rows] + cf[1, x, pl.ds(r - 1, size)])
+                               + (k + d))
+            return 0
+
+        lax.fori_loop(x0, x0 + n, body, 0, unroll=8 if n > 1 else 1)
 
     def everywhere(fn):
         def body(x, _):
             fn(x, pl.ds(OY - 8, BY + 16))
             return 0
-        lax.fori_loop(0, EX, body, 0, unroll=4)
+        lax.fori_loop(0, NX, body, 0, unroll=4)
 
     def block(fn, unroll=4):
         def body(x, _):
@@ -355,17 +478,22 @@
             return 0
         lax.fori_loop(OX, OX + BX, body, 0, unroll=unroll)
 
-    inner_part(functools.partial(laplacian, y4, w4), 1)
+    inner_part(y4, to_w(w4), 1, advect=False)
+    prepare_s()
+    prepare_d(OX, BX, OY, BY)
     finish(moved)
     finish(later)
-    laplacian(y4, w4, OX - 1, 2, WIDE, 2)
-    laplacian(y4, w4, OX + BX - 1, 2, WIDE, 2)
-    laplacian(y4, w4, OX + 1, BX - 2, ((OY - 8, 16), (BOT - 8, 16)), BX)
+    blocks(y4, OX - 1, 2, 2, WIDE, to_w(w4), advect=False)
+    blocks(y4, OX + BX - 1, 2, 2, WIDE, to_w(w4), advect=False)
+    blocks(y4, OX + 1, BX - 2, 5, ((OY - 8, 16), (BOT - 8, 16)), to_w(w4), advect=False)
     clear_outside(w4)
-    parts = moments(y4, w4)
     pl.semaphore_wait(in_sem, len(GROUP_B))
-    send_sums(0, parts)
-    moved = advance(y4, w4, qr4, g4, 0)
+    send_sums(0, moments(y4, w4))
+    moved = advance(y4, w4, qr4, g4)
+    prepare_d(OX - 1, 1, OY, BY)
+    prepare_d(OX + BX, 1, OY, BY)
+    prepare_d(OX, BX, OY - 8, 8)
+    prepare_d(OX, BX, BOT, 8)
     finish(moved)
     a4, c4 = solve(0)
 
@@ -375,7 +503,19 @@
         qr3[2, x, rows] = (1.4 * y4[x, rows] + a * (0.6 * qr4[0, x, rows] - 0.2 * w4[x, rows])
                            + c * (0.6 * qr4[1, x, rows] + 0.2 * g4[x, rows]))
 
-    block(base2)
+    def few(x0, n):
+        for i in range(n):
+            base2(x0 + i, pl.ds(OY, BY))
+
+    def strips(i, _):
+        for k in range(7):
+            base2(OX + 2 + 7 * i + k, pl.ds(OY, 8))
+            base2(OX + 2 + 7 * i + k, pl.ds(BOT - 8, 8))
+        return 0
+
+    few(OX, 2)
+    few(OX + BX - 2, 2)
+    lax.fori_loop(0, 4, strips, 0)
     moved2 = swap(qr3, (2,))
 
     def make_y3(x, rows):
@@ -383,10 +523,11 @@
         y3[x, rows] = y4[x, rows] + a * qr4[0, x, rows] + c * qr4[1, x, rows]
 
     everywhere(make_y3)
-    laplacian(y3, w3, OX - 1, BX + 2, WIDE, 4)
+    laplacian7(y3, w3)
     clear_outside(w3)
     send_sums(1, moments(y3, w3))
-    moved = advance(y3, w3, qr3, g3, 1)
+    moved = advance(y3, w3, qr3, g3)
+    lax.fori_loop(OX + 2, OX + BX - 2, lambda x, _: (base2(x, pl.ds(OY + 8, BY - 16)), 0)[1], 0, unroll=4)
     finish(moved2)
     finish(moved)
     a3, c3 = solve(1)
@@ -396,18 +537,18 @@
         y2[x, rows] = qr3[2, x, rows] + a * qr3[0, x, rows] + c * qr3[1, x, rows]
 
     everywhere(make_y2)
-    laplacian(y2, w2, OX - 1, BX + 2, WIDE, 4)
+    laplacian7(y2, w2)
     clear_outside(w2)
     send_sums(2, moments(y2, w2))
 
-    def emit_t1(x, rows, v, fv, dv):
-        t1[x - OX, pl.ds(rows.start - OY, rows.size)] = v + 0.5 * fv - 0.25 * w2[x, rows]
-
-    def emit_t2(x, rows, v, fv, dv):
-        t2[x - OX, pl.ds(rows.start - OY, rows.size)] = v + 0.5 * fv + 0.25 * dv
-
-    stencil(y2, OX, BX, WHOLE, emit_t1, diffuse=False, unroll=4)
-    stencil(w2, OX, BX, WHOLE, emit_t2, unroll=4)
+    def emit_t1(x, px, r, size, v, sv):
+        put(t1, x, px, r, size, v + sv, -OX, -OY)
+
+    def emit_t2(x, px, r, size, v, sv):
+        put(t2, x, px, r, size, v + sv, -OX, -OY)
+
+    sweep7(y2, OX, BX, HALVES, (s_weights,), emit_t1, UNROLL[2])
+    sweep7(w2, OX, BX, HALVES, (s_weights,), emit_t2, UNROLL[2])
 
     def base1(x, rows):
         size = rows.size
@@ -421,20 +562,11 @@
 
     block(base1)
     a2, c2 = solve(2)
-    stores = []
-    for k in range(4):
-        planes = pl.ds(8 * k, 8)
-
-        def body(x, _):
-            b1[x] = b1[x] + full(a2, BY) * t1[x] + full(c2, BY) * t2[x]
-            return 0
-
-        lax.fori_loop(8 * k, 8 * k + 8, body, 0, unroll=4)
-        store = pltpu.make_async_copy(b1.at[planes], out.at[planes], out_sem.at[k])
-        store.start()
-        stores.append(store)
-    for store in stores:
-        store.wait()
+    def body(x, _):
+        out[x] = b1[x] + full(a2, BY) * t1[x] + full(c2, BY) * t2[x]
+        return 0
+
+    lax.fori_loop(0, BX, body, 0, unroll=8)
 
 
 COPIES = 80
@@ -453,16 +585,15 @@
         name="adjoint_step",
         out_shape=jax.ShapeDtypeStruct((BX, BY, BZ), F32),
         in_specs=[anywhere, anywhere, anywhere, pl.BlockSpec(memory_space=pltpu.VMEM)],
-        out_specs=anywhere,
+        out_specs=pl.BlockSpec(memory_space=pltpu.VMEM),
         scratch_shapes=[
             ext, stack(3), stack(3), ext, ext, ext, stack(2), ext, ext, ext, stack(3), ext, ext,
-            plain, plain, plain, pltpu.VMEM((128, 128), F32), pltpu.VMEM((3, 128, BZ), F32),
+            plain, plain, plain, pltpu.VMEM((7, BX, BY, BZ), F32), ext, ext, ext, pltpu.VMEM((128, 128), F32), pltpu.VMEM((3, 128, BZ), F32),
             pltpu.SemaphoreType.DMA((7,)), pltpu.SemaphoreType.DMA((COPIES,)), pltpu.SemaphoreType.DMA((COPIES,)),
             pltpu.SemaphoreType.DMA((3,)), pltpu.SemaphoreType.DMA((3,)), pltpu.SemaphoreType.REGULAR,
-            pltpu.SemaphoreType.DMA((4,)),
         ],
         compiler_params=pltpu.CompilerParams(
-            collective_id=0, has_side_effects=True, vmem_limit_bytes=60 * 1024 * 1024),
+            collective_id=0, has_side_effects=True, vmem_limit_bytes=57 * 1024 * 1024),
     )(cotangent, speed, coeff, dirs)
 
 

time: 61.3 us -> 55.5 us (0.905)
  Pallas kernels: 58.8 us -> 53 us
    pallas_call x1, Pallas kernels: 58.8 us -> 53 us  [local(): pl.pallas_call(kernel, name='adjoint_step', out_shape=jax.ShapeDtypeStruc...]
where the time goes in v2:
time: 55.5 us; the launch traced here: 55.3 us
  Pallas kernels  53 us (95%)
  local copies, waits for them, and re-layouts  2.31 us (4%)
    pallas_call x1, Pallas kernels, local(): pl.pallas_call(kernel, name='adjoint_step', out_shape=jax.ShapeDtypeStruc...  53 us
    unnamed x1, local copies, waits for them, and re-layouts  2.31 us

profile of v2, /device:TPU:1, one launch (start us, length us, event | category | flops | bytes accessed | tf_op | source)
XLA Modules:
  0.0 55.3 jit_solution(17971426713475576575)
XLA Ops:
  0.0 53.0 %adjoint_step.1 = f32[32,64,128]{2,1,0:T(8,128)} custom-call(f32[32,64,128]{2,1,0:T(8,128)} %cot.1, f32[3,32,64,128]{3,2,1,0:T(8,128)} %speed.1, f32[3,32,64,128]{3,2,1,0:T(8,128)} %coeff.1, s32[3,32,64]{2,1,0:T(8,128)} %dirs.1), custom_call_target="tpu_custom_call" | custom-call | tf_op jit(solution)/shard_map/adjoint_step/pallas_call | solution.py:583
  53.0 2.3 %copy.6 = f32[32,64,128]{2,1,0:T(8,128)} copy(f32[32,64,128]{2,1,0:T(8,128)} %adjoint_step.1) | data formatting | bytes 2097152

commit v3 on v2

--- a/solution.py
+++ b/solution.py
@@ -46,7 +46,7 @@
 
 
 def kernel(cot, speed, coeff, dirs, out, cfield, cf, vel, y4, w4, g4, qr4, y3, w3, g3, qr3, y2, w2, t1, t2, b1, sc, up_z, down_z, centre,
-           signs, sums, load_sem, send, recv, ar_send, ar_recv, in_sem):
+           ways, signs, sums, load_sem, send, recv, ar_send, ar_recv, in_sem):
     gx, gy = lax.axis_index("gx"), lax.axis_index("gy")
     place = {"zl": gx // 4, "y": gx % 4, "x": gy // 4, "zh": (gy // 2) % 2, "c": gy % 2}
 
@@ -76,8 +76,9 @@
         loads.append(pltpu.make_async_copy(speed.at[d], vel.at[(d, *inner)], load_sem.at[1 + d]))
     for d in range(3):
         loads.append(pltpu.make_async_copy(coeff.at[d], cf.at[(d, *inner)], load_sem.at[4 + d]))
-    for load in loads:
-        load.start()
+    loads.append(pltpu.make_async_copy(dirs, ways, load_sem.at[7]))
+    for k in (7, 1, 2, 0, 4, 5, 6, 3):
+        loads[k].start()
 
     zero_rim(cfield)
     for d in range(3):
@@ -98,20 +99,22 @@
         zero_rim(qr3, k)
 
     signs[...] = jnp.zeros((128, 128), F32)
+    loads[7].wait()
     for d in range(3):
-        signs[pl.ds(32 * d, 32), pl.ds(0, 64)] = (1 - 2 * dirs[d]).astype(F32)
+        signs[pl.ds(32 * d, 32), pl.ds(0, 64)] = (1 - 2 * ways[d]).astype(F32)
     signs[...] = signs[...].T
-    for load in loads[1:4]:
-        load.wait()
-    columns = signs[pl.ds(0, 64), :]
-    for d in range(3):
-        for x in range(BX):
-            k = 32 * d + x
-            rows = pl.ds(OY, BY)
-            vel[d, OX + x, rows] = vel[d, OX + x, rows] * columns[:, k:k + 1]
-    loads[0].wait()
-    for load in loads[4:]:
-        load.wait()
+
+    def sign(d, x, r, size):
+        rows, k = pl.ds(OY + r, size), 32 * d + x
+        vel[d, OX + x, rows] = vel[d, OX + x, rows] * signs[pl.ds(r, size), k:k + 1]
+
+    loads[1].wait()
+    sign(0, BX - 1, 0, BY)
+    loads[2].wait()
+    for x in range(BX):
+        sign(1, x, BY - 8, 8)
+    for k in (0, 4, 5, 6):
+        loads[k].wait()
 
     count = [0]
     edges = {-1: (gx > 0, gy > 0), 1: (gx < 7, gy < 15)}
@@ -281,6 +284,12 @@
              corner(cf, (pl.ds(0, 2),), 1, 1), corner(cf, (1,), -1, 1), corner(cf, (0,), 1, -1)]
     for o in GROUP_B:
         pl.semaphore_signal(in_sem, inc=1, device_id=device(o), device_id_type=MESH)
+    loads[3].wait()
+    for x in range(BX):
+        if x < BX - 1:
+            sign(0, x, 0, BY)
+        sign(1, x, 0, BY - 8)
+        sign(2, x, 0, BY)
     inner_part(cfield, emit_y4, 1)
     finish(first)
     rim(cfield, emit_y4, 1)
@@ -408,7 +417,7 @@
     def put(ref, x, px, r, size, value, dx=0, dr=0):
         ref[pl.ds(x + dx, px), pl.ds(r + dr, size)] = value.reshape(px, size, BZ)
 
-    def advance(y, w, qr, g):
+    def advance(y, w, qr, g, r):
         def emit_q(x, px, r, size, v, sv):
             put(qr.at[0], x, px, r, size, sv)
 
@@ -423,8 +432,10 @@
 
         both = (s_weights, d_weights)
         rim7(y, (s_weights,), emit_q)
+        copies = swap(qr, (0,))
+        send_sums(r, moments(y, w))
         rim7(w, both, emit_r)
-        copies = swap(qr, (pl.ds(0, 2),))
+        copies += swap(qr, (1,))
         sweep7(y, OX + 2, BX - 4, CORE, (s_weights,), emit_q, UNROLL[0])
         sweep7(w, OX + 2, BX - 4, CORE, both, emit_r, UNROLL[0])
         return copies
@@ -488,8 +499,7 @@
     blocks(y4, OX + 1, BX - 2, 5, ((OY - 8, 16), (BOT - 8, 16)), to_w(w4), advect=False)
     clear_outside(w4)
     pl.semaphore_wait(in_sem, len(GROUP_B))
-    send_sums(0, moments(y4, w4))
-    moved = advance(y4, w4, qr4, g4)
+    moved = advance(y4, w4, qr4, g4, 0)
     prepare_d(OX - 1, 1, OY, BY)
     prepare_d(OX + BX, 1, OY, BY)
     prepare_d(OX, BX, OY - 8, 8)
@@ -525,8 +535,7 @@
     everywhere(make_y3)
     laplacian7(y3, w3)
     clear_outside(w3)
-    send_sums(1, moments(y3, w3))
-    moved = advance(y3, w3, qr3, g3)
+    moved = advance(y3, w3, qr3, g3, 1)
     lax.fori_loop(OX + 2, OX + BX - 2, lambda x, _: (base2(x, pl.ds(OY + 8, BY - 16)), 0)[1], 0, unroll=4)
     finish(moved2)
     finish(moved)
@@ -584,12 +593,12 @@
         kernel,
         name="adjoint_step",
         out_shape=jax.ShapeDtypeStruct((BX, BY, BZ), F32),
-        in_specs=[anywhere, anywhere, anywhere, pl.BlockSpec(memory_space=pltpu.VMEM)],
+        in_specs=[anywhere] * 4,
         out_specs=pl.BlockSpec(memory_space=pltpu.VMEM),
         scratch_shapes=[
             ext, stack(3), stack(3), ext, ext, ext, stack(2), ext, ext, ext, stack(3), ext, ext,
-            plain, plain, plain, pltpu.VMEM((7, BX, BY, BZ), F32), ext, ext, ext, pltpu.VMEM((128, 128), F32), pltpu.VMEM((3, 128, BZ), F32),
-            pltpu.SemaphoreType.DMA((7,)), pltpu.SemaphoreType.DMA((COPIES,)), pltpu.SemaphoreType.DMA((COPIES,)),
+            plain, plain, plain, pltpu.VMEM((7, BX, BY, BZ), F32), ext, ext, ext, pltpu.VMEM((3, BX, BY), jnp.int32), pltpu.VMEM((128, 128), F32), pltpu.VMEM((3, 128, BZ), F32),
+            pltpu.SemaphoreType.DMA((8,)), pltpu.SemaphoreType.DMA((COPIES,)), pltpu.SemaphoreType.DMA((COPIES,)),
             pltpu.SemaphoreType.DMA((3,)), pltpu.SemaphoreType.DMA((3,)), pltpu.SemaphoreType.REGULAR,
         ],
         compiler_params=pltpu.CompilerParams(

time: 55.5 us -> 53.3 us (0.960)
  Pallas kernels: 53 us -> 50.8 us
    pallas_call x1, Pallas kernels: 53 us -> 50.8 us  [local(): pl.pallas_call(kernel, name='adjoint_step', out_shape=jax.ShapeDtypeStruc...]
where the time goes in v3:
time: 53.3 us; the launch traced here: 53.2 us
  Pallas kernels  50.8 us (95%)
  local copies, waits for them, and re-layouts  2.31 us (4%)
    pallas_call x1, Pallas kernels, local(): pl.pallas_call(kernel, name='adjoint_step', out_shape=jax.ShapeDtypeStruc...  50.8 us
    unnamed x1, local copies, waits for them, and re-layouts  2.31 us

profile of v3, /device:TPU:1, one launch (start us, length us, event | category | flops | bytes accessed | tf_op | source)
XLA Modules:
  0.0 53.2 jit_solution(1907933753079618514)
XLA Ops:
  0.0 50.8 %adjoint_step.1 = f32[32,64,128]{2,1,0:T(8,128)} custom-call(f32[32,64,128]{2,1,0:T(8,128)} %cot.1, f32[3,32,64,128]{3,2,1,0:T(8,128)} %speed.1, f32[3,32,64,128]{3,2,1,0:T(8,128)} %coeff.1, s32[3,32,64]{2,1,0:T(8,128)} %dirs.1), custom_call_target="tpu_custom_call" | custom-call | tf_op jit(solution)/shard_map/adjoint_step/pallas_call | solution.py:592
  50.8 2.3 %copy.6 = f32[32,64,128]{2,1,0:T(8,128)} copy(f32[32,64,128]{2,1,0:T(8,128)} %adjoint_step.1) | data formatting | bytes 2097152

commit v4 on v3

--- a/solution.py
+++ b/solution.py
@@ -425,6 +425,12 @@
             put(qr.at[1], x, px, r, size, sv)
             put(g, x, px, r, size, dv)
 
+        def emit_s(x, px, r, size, v, sv):
+            put(qr.at[1], x, px, r, size, sv)
+
+        def emit_g(x, px, r, size, v, dv):
+            put(g, x, px, r, size, dv)
+
         def rim7(src, weights, emit):
             blocks7(src, OX, 2, 2, HALVES, weights, emit)
             blocks7(src, OX + BX - 2, 2, 2, HALVES, weights, emit)
@@ -434,8 +440,11 @@
         rim7(y, (s_weights,), emit_q)
         copies = swap(qr, (0,))
         send_sums(r, moments(y, w))
-        rim7(w, both, emit_r)
+        rim7(w, (s_weights,), emit_s)
         copies += swap(qr, (1,))
+        if r == 0:
+            prepare_d(OX, BX, OY, BY)
+        rim7(w, (d_weights,), emit_g)
         sweep7(y, OX + 2, BX - 4, CORE, (s_weights,), emit_q, UNROLL[0])
         sweep7(w, OX + 2, BX - 4, CORE, both, emit_r, UNROLL[0])
         return copies
@@ -491,7 +500,6 @@
 
     inner_part(y4, to_w(w4), 1, advect=False)
     prepare_s()
-    prepare_d(OX, BX, OY, BY)
     finish(moved)
     finish(later)
     blocks(y4, OX - 1, 2, 2, WIDE, to_w(w4), advect=False)

time: 53.3 us -> 53.2 us (level)
  no operation moved by 1% of the time
where the time goes in v4:
time: 53.2 us; the launch traced here: 53.1 us
  Pallas kernels  50.8 us (95%)
  local copies, waits for them, and re-layouts  2.31 us (4%)
    pallas_call x1, Pallas kernels, local(): pl.pallas_call(kernel, name='adjoint_step', out_shape=jax.ShapeDtypeStruc...  50.8 us
    unnamed x1, local copies, waits for them, and re-layouts  2.31 us

profile of v4, /device:TPU:1, one launch (start us, length us, event | category | flops | bytes accessed | tf_op | source)
XLA Modules:
  0.0 53.1 jit_solution(13905955388005072253)
XLA Ops:
  0.0 50.8 %adjoint_step.1 = f32[32,64,128]{2,1,0:T(8,128)} custom-call(f32[32,64,128]{2,1,0:T(8,128)} %cot.1, f32[3,32,64,128]{3,2,1,0:T(8,128)} %speed.1, f32[3,32,64,128]{3,2,1,0:T(8,128)} %coeff.1, s32[3,32,64]{2,1,0:T(8,128)} %dirs.1), custom_call_target="tpu_custom_call" | custom-call | tf_op jit(solution)/shard_map/adjoint_step/pallas_call | solution.py:600
  50.8 2.3 %copy.6 = f32[32,64,128]{2,1,0:T(8,128)} copy(f32[32,64,128]{2,1,0:T(8,128)} %adjoint_step.1) | data formatting | bytes 2097152
